TPU v7x, 32 devices: a whole 2x2x4 slice. The times are simulated.
32 devices in a mesh: chain: 16 (over z, x, core), shard: 2 (over y).
Axes of the slice: x: 2, y: 2, z: 4, core: 2. Of those that a mesh axis runs over, the one named last changes fastest.
Arguments:
- w_pair: bfloat16 [16, 2, 256, 4096], P('chain', None, 'shard'), may hold values from -6 to 6
- w_down: bfloat16 [16, 256, 4096], P('chain', 'shard'), may hold values from -6 to 6
- tokens: bfloat16 [16, 512, 4096], P('chain', 'shard'), may hold values from -6 to 6
- cotangent: bfloat16 [16, 512, 4096], P('chain', 'shard'), may hold values from -6 to 6
- seq_ids: int32 [16, 512], P('chain', 'shard'), may hold values from 0 to 7, never falling along the last dimension, each value on 1 to 128 neighbouring positions
- msg_left: bfloat16 [16, 2, 256, 4096], P('chain', None, 'shard'), may hold values from -9 to 9
- msg_right: bfloat16 [16, 2, 256, 4096], P('chain', None, 'shard'), may hold values from -9 to 9
- count_left: int32 [16], P('chain'), may hold values from 0 to 5, as said below
- count_right: int32 [16], P('chain'), may hold values from 0 to 5, as said below
Outputs:
- new_pair: bfloat16 [16, 2, 256, 4096], P('chain', None, 'shard')
Inputs may be any that keep to these rules, and one draw needn't show every extreme that they name: count_left of worker w is at most min(w, 5); some worker at least 5 from both ends of the chain has count_left equal to 5. count_right of worker w is at most min(15 - w, 5); the same worker has count_right equal to 5.
All inputs are finite; a program needn't handle non-finite values.
Results may differ from a plain program's by a relative error of at most 0.0053.
Values may be sent and summed in bfloat16 or wider, within the bound.
No kernel may reach another device: no remote copies, remote signals or barrier semaphores. Data moves between devices by JAX's collectives and lax.ppermute only.
A program may use at most 128 MiB of HBM per device.

v0:
```python
import jax
import jax.numpy as jnp
from jax import lax
from jax.sharding import PartitionSpec as P

D = 4096
SEQS = 8


learn_rate = 1.0


def passed_along(shard, axis, by):
    peers = lax.axis_size(axis)
    pairs = [(i, i + by) for i in range(peers) if 0 <= i + by < peers]
    return lax.ppermute(shard, axis, pairs)


def body(w_pair, w_down, tokens, cotangent, seq_ids, msg_left, msg_right, count_left, count_right):
    tok_rows, cot_rows, id_wire = (
        lax.all_gather(tokens[0], "shard", axis=0, tiled=True),
        lax.all_gather(cotangent[0], "shard", axis=0, tiled=True),
        lax.all_gather(seq_ids[0].astype(jnp.bfloat16), "shard", axis=0, tiled=True),
    )
    segment_ids = id_wire.astype(jnp.int32)
    total_rows = tok_rows.shape[0]
    width_scale = D ** (-0.5)
    pair_local = w_pair[0]
    contract_last = (((1,), (1,)), ((), ()))
    gate_pre = (
        lax.dot_general(tok_rows, pair_local[0], contract_last, preferred_element_type=jnp.float32)
        * width_scale
    )
    up_pre = (
        lax.dot_general(tok_rows, pair_local[1], contract_last, preferred_element_type=jnp.float32)
        * width_scale
    )
    one_hot = (segment_ids[:, None] == jnp.arange(SEQS, dtype=jnp.int32)[None, :]).astype(
        jnp.float32
    )
    seq_count = jnp.sum(one_hot, axis=0)
    seq_len = jnp.sum(one_hot * seq_count[None, :], axis=1)
    tok_weight = total_rows / SEQS / seq_len
    scaled_cot = (tok_weight[:, None] * cot_rows.astype(jnp.float32)).astype(jnp.bfloat16)
    grad_hidden = (
        lax.dot_general(scaled_cot, w_down[0], contract_last, preferred_element_type=jnp.float32)
        * width_scale
    )
    sigmoid_gate = jax.nn.sigmoid(gate_pre)
    grad_gate = (
        grad_hidden * up_pre * sigmoid_gate * (1.0 + gate_pre * (1.0 - sigmoid_gate))
    ).astype(jnp.bfloat16)
    grad_up = (grad_hidden * gate_pre * sigmoid_gate).astype(jnp.bfloat16)
    batch_scale = total_rows ** (-0.5)
    contract_tokens = (((0,), (0,)), ((), ()))
    out_right_count = (1 + count_left).astype(jnp.bfloat16)
    out_left_count = (1 + count_right).astype(jnp.bfloat16)
    block_count = 4
    block_width = D // block_count
    results = []
    for block_index in range(block_count):
        first_col = block_index * block_width
        tok_cols = tok_rows[:, first_col : first_col + block_width]
        gate_part = lax.dot_general(
            grad_gate, tok_cols, contract_tokens, preferred_element_type=jnp.float32
        )
        up_part = lax.dot_general(
            grad_up, tok_cols, contract_tokens, preferred_element_type=jnp.float32
        )
        half_block = pair_local[:, :, first_col : first_col + block_width].astype(
            jnp.float32
        ) - learn_rate * (jnp.stack([gate_part, up_part]) * batch_scale)
        send_right = (
            half_block + msg_left[0][:, :, first_col : first_col + block_width].astype(jnp.float32)
        ).astype(jnp.bfloat16)
        send_left = (
            half_block + msg_right[0][:, :, first_col : first_col + block_width].astype(jnp.float32)
        ).astype(jnp.bfloat16)
        recv_left, cnt_left = passed_along((send_right, out_right_count), "chain", 1)
        recv_right, cnt_right = passed_along((send_left, out_left_count), "chain", -1)
        total_count = 1.0 + cnt_left.astype(jnp.float32) + cnt_right.astype(jnp.float32)
        results.append(
            (half_block + recv_left.astype(jnp.float32) + recv_right.astype(jnp.float32))
            / total_count
        )
    updated = jnp.concatenate(results, axis=2)
    return updated.astype(jnp.bfloat16)[None]


def solution(mesh):
    return jax.shard_map(
        body,
        mesh=mesh,
        in_specs=(
            P("chain", None, "shard", None),
            P("chain", "shard", None),
            P("chain", "shard", None),
            P("chain", "shard", None),
            P("chain", "shard"),
            P("chain", None, "shard", None),
            P("chain", None, "shard", None),
            P("chain"),
            P("chain"),
        ),
        out_specs=P("chain", None, "shard", None),
        check_vma=False,
    )
```

profile of v0, /device:TPU:9, one launch (start us, length us, event | category | flops | bytes accessed | tf_op | source)
XLA Modules:
  0.0 202.3 jit_solution(10085506342924397055)
XLA Ops:
  6.5 0.7 all-gather.8.cloned.1.call-update
  7.3 0.7 all-gather.6.cloned.1.call-update
  8.0 3.1 %all-gather = bf16[1,512]{1,0:T(2,128)(2,1)S(1)} all-gather(bf16[1,256]{1,0:T(2,128)(2,1)S(1)} %convert_element_type.135), channel_id=2, replica_groups=mesh['chain'=16,'shard'=2] {'shard'}, dimensions={1}, use_global_device_ids=true | all-gather | bytes 1536 | tf_op jit(solution)/shard_map/all_gather | solution.py:23
  11.3 55.3 %all-gather.8.cloned.1.call-done = bf16[1,512,4096]{2,1,0:T(8,128)(2,1)} async-done(((bf16[1,256,4096]{2,1,0:T(8,128)(2,1)}), bf16[1,512,4096]{2,1,0:T(8,128)(2,1)}) %all-gather.8.cloned.1.call-update) | async-done | bytes 4194320 | tf_op jit(solution)/shard_map/all_gather | solution.py:21
  66.6 3.4 %convolution_multiply_fusion = f32[512,128]{1,0:T(8,128)S(1)} fusion(bf16[1,2,128,4096]{3,2,1,0:T(8,128)(2,1)S(1)} %copy-done.1, bf16[1,512,4096]{2,1,0:T(8,128)(2,1)} %all-gather.8.cloned.1.call-done), kind=kOutput, calls=%fused_computation.14 | convolution fusion | flops 536936448 | bytes 5505024 | tf_op jit(solution)/shard_map/dot_general | solution.py:31
  70.1 54.8 %all-gather.6.cloned.1.call-done = bf16[1,512,4096]{2,1,0:T(8,128)(2,1)} async-done(((bf16[1,256,4096]{2,1,0:T(8,128)(2,1)}), bf16[1,512,4096]{2,1,0:T(8,128)(2,1)}) %all-gather.6.cloned.1.call-update) | async-done | bytes 4194320 | tf_op jit(solution)/shard_map/all_gather | solution.py:22
  124.9 3.6 %multiply_convert_fusion = (bf16[512,128]{1,0:T(8,128)(2,1)S(1)}, f32[512,128]{1,0:T(8,128)S(1)}) fusion(f32[512,128]{1,0:T(8,128)S(1)} %convolution_multiply_fusion, bf16[1,128,4096]{2,1,0:T(8,128)(2,1)S(1)} %copy-done, bf16[1,512,4096]{2,1,0:T(8,128)(2,1)} %all-gather.6.cloned.1.call-done, f32[512]{0:T(512)S(1)} %broadcast_divide_fusion), kind=kOutput, calls=%fused_computation.58 | convolution fusion | flops 543621120 | bytes 5900288 | tf_op jit(solution)/shard_map/dot_general | solution.py:46
  128.6 1.3 fusion.11
  129.9 0.3 convolution_bitcast_fusion.1
  130.2 0.3 convolution_bitcast_fusion.3
  130.5 0.3 convolution_bitcast_fusion.5
  130.9 0.3 convolution_bitcast_fusion.7
  131.2 0.3 convolution_bitcast_fusion
  131.5 0.3 convolution_bitcast_fusion.2
  131.9 0.3 convolution_bitcast_fusion.4
  132.2 0.3 convolution_bitcast_fusion.6
  132.6 1.3 add_convert_fusion.6
  133.8 2.8 %collective-permute-start.1 = (bf16[2,128,1024]{2,1,0:T(8,128)(2,1)S(1)}, bf16[2,128,1024]{2,1,0:T(8,128)(2,1)S(1)}, u32[]{:S(2)}, u32[]{:S(2)}) collective-permute-start(bf16[2,128,1024]{2,1,0:T(8,128)(2,1)S(1)} %get-tuple-element.9), channel_id=1, source_target_pairs={{2,0},{4,2},{6,4},{8,6},{10,8},{12,10},{14,12},{16,14},{18,16},{20... | collective-permute-start | bytes 1572872 | tf_op jit(solution)/shard_map/ppermute | solution.py:16
  136.6 2.6 %collective-permute-start.9 = (bf16[2,128,1024]{2,1,0:T(8,128)(2,1)S(1)}, bf16[2,128,1024]{2,1,0:T(8,128)(2,1)S(1)}, u32[]{:S(2)}, u32[]{:S(2)}) collective-permute-start(bf16[2,128,1024]{2,1,0:T(8,128)(2,1)S(1)} %get-tuple-element.10), channel_id=1, source_target_pairs={{2,0},{4,2},{6,4},{8,6},{10,8},{12,10},{14,12},{16,14},{18,16},{20... | collective-permute-start | bytes 1572872 | tf_op jit(solution)/shard_map/ppermute | solution.py:16
  139.2 1.3 add_convert_fusion.7
  140.5 3.0 %collective-permute-start.8 = (bf16[2,128,1024]{2,1,0:T(8,128)(2,1)S(1)}, bf16[2,128,1024]{2,1,0:T(8,128)(2,1)S(1)}, u32[]{:S(2)}, u32[]{:S(2)}) collective-permute-start(bf16[2,128,1024]{2,1,0:T(8,128)(2,1)S(1)} %get-tuple-element.6), channel_id=1, source_target_pairs={{0,2},{2,4},{4,6},{6,8},{8,10},{10,12},{12,14},{14,16},{16,18},{18... | collective-permute-start | bytes 1572872 | tf_op jit(solution)/shard_map/ppermute | solution.py:16
  144.1 11.7 %collective-permute-start.2 = (bf16[1]{0:T(256)(128)(2,1)}, bf16[1]{0:T(256)(128)(2,1)}, u32[]{:S(2)}, u32[]{:S(2)}) collective-permute-start(bf16[1]{0:T(256)(128)(2,1)} %convert_element_type.149), channel_id=1, source_target_pairs={{0,2},{2,4},{4,6},{6,8},{8,10},{10,12},{12,14},{14,16},{16,18},{18... | collective-permute-start | bytes 14 | tf_op jit(solution)/shard_map/ppermute | solution.py:16
  156.5 2.9 %collective-permute-start.3 = (bf16[1]{0:T(256)(128)(2,1)}, bf16[1]{0:T(256)(128)(2,1)}, u32[]{:S(2)}, u32[]{:S(2)}) collective-permute-start(bf16[1]{0:T(256)(128)(2,1)} %convert_element_type.151), channel_id=1, source_target_pairs={{2,0},{4,2},{6,4},{8,6},{10,8},{12,10},{14,12},{16,14},{18,16},{20... | collective-permute-start | bytes 14 | tf_op jit(solution)/shard_map/ppermute | solution.py:16
  159.3 1.9 collective-permute-start.7
  161.3 1.9 collective-permute-start.5
  163.2 3.9 %collective-permute-start = (bf16[2,128,1024]{2,1,0:T(8,128)(2,1)S(1)}, bf16[2,128,1024]{2,1,0:T(8,128)(2,1)S(1)}, u32[]{:S(2)}, u32[]{:S(2)}) collective-permute-start(bf16[2,128,1024]{2,1,0:T(8,128)(2,1)S(1)} %get-tuple-element.5), channel_id=1, source_target_pairs={{0,2},{2,4},{4,6},{6,8},{8,10},{10,12},{12,14},{14,16},{16,18},{18... | collective-permute-start | bytes 1572872 | tf_op jit(solution)/shard_map/ppermute | solution.py:16
  167.2 2.4 %collective-permute-start.6 = (bf16[2,128,1024]{2,1,0:T(8,128)(2,1)S(1)}, bf16[2,128,1024]{2,1,0:T(8,128)(2,1)S(1)}, u32[]{:S(2)}, u32[]{:S(2)}) collective-permute-start(bf16[2,128,1024]{2,1,0:T(8,128)(2,1)S(1)} %get-tuple-element.7), channel_id=1, source_target_pairs={{0,2},{2,4},{4,6},{6,8},{8,10},{10,12},{12,14},{14,16},{16,18},{18... | collective-permute-start | bytes 1572872 | tf_op jit(solution)/shard_map/ppermute | solution.py:16
  169.6 4.5 %collective-permute-start.4 = (bf16[2,128,1024]{2,1,0:T(8,128)(2,1)S(1)}, bf16[2,128,1024]{2,1,0:T(8,128)(2,1)S(1)}, u32[]{:S(2)}, u32[]{:S(2)}) collective-permute-start(bf16[2,128,1024]{2,1,0:T(8,128)(2,1)S(1)} %get-tuple-element.8), channel_id=1, source_target_pairs={{0,2},{2,4},{4,6},{6,8},{8,10},{10,12},{12,14},{14,16},{16,18},{18... | collective-permute-start | bytes 1572872 | tf_op jit(solution)/shard_map/ppermute | solution.py:16
  175.3 0.4 fusion.32
  175.7 16.9 %collective-permute-done.5 = bf16[2,128,1024]{2,1,0:T(8,128)(2,1)S(1)} collective-permute-done((bf16[2,128,1024]{2,1,0:T(8,128)(2,1)S(1)}, bf16[2,128,1024]{2,1,0:T(8,128)(2,1)S(1)}, u32[]{:S(2)}, u32[]{:S(2)}) %collective-permute-start.5) | collective-permute-done | bytes 524320 | tf_op jit(solution)/shard_map/ppermute | solution.py:16
  192.6 1.3 fusion.29
  194.0 1.5 pad_maximum_fusion
  (28 shorter events, 0.4 us)
Async XLA Ops:
  6.5 118.4 %copy-start = (bf16[1,128,4096]{2,1,0:T(8,128)(2,1)S(1)}, bf16[1,128,4096]{2,1,0:T(8,128)(2,1)}, u32[]{:S(2)}) copy-start(bf16[1,128,4096]{2,1,0:T(8,128)(2,1)} %param.10) | copy-start | bytes 3145732
  6.5 1.5 copy-start.5
  6.5 60.1 %copy-start.1 = (bf16[1,2,128,4096]{3,2,1,0:T(8,128)(2,1)S(1)}, bf16[1,2,128,4096]{3,2,1,0:T(8,128)(2,1)}, u32[]{:S(2)}) copy-start(bf16[1,2,128,4096]{3,2,1,0:T(8,128)(2,1)} %param.9) | copy-start | bytes 6291460
  6.5 60.1 %all-gather.8.cloned.1.call-start = ((), (), s32[]{:S(2)}) async-start(), calls=%async_computation.1 | async-start | bytes 6291456 | tf_op jit(solution)/shard_map/all_gather | solution.py:21
  7.3 117.7 %all-gather.6.cloned.1.call-start = ((), (), s32[]{:S(2)}) async-start(), calls=%async_computation | async-start | bytes 6291456 | tf_op jit(solution)/shard_map/all_gather | solution.py:22
  124.9 3.7 %copy-start.2 = (bf16[1,512,4096]{2,1,0:T(8,128)(2,1)S(1)}, bf16[1,512,4096]{2,1,0:T(8,128)(2,1)}, u32[]{:S(2)}) copy-start(bf16[1,512,4096]{2,1,0:T(8,128)(2,1)} %all-gather.8.cloned.1.call-done) | copy-start | bytes 12582916
  130.9 1.7 copy-start.3
  132.5 6.7 %copy-start.4 = (bf16[1,2,128,4096]{3,2,1,0:T(8,128)(2,1)S(1)}, bf16[1,2,128,4096]{3,2,1,0:T(8,128)(2,1)}, u32[]{:S(2)}) copy-start(bf16[1,2,128,4096]{3,2,1,0:T(8,128)(2,1)} %param.14) | copy-start | bytes 6291460
  133.8 29.4 %collective-permute-start.1 = (bf16[2,128,1024]{2,1,0:T(8,128)(2,1)S(1)}, bf16[2,128,1024]{2,1,0:T(8,128)(2,1)S(1)}, u32[]{:S(2)}, u32[]{:S(2)}) collective-permute-start(bf16[2,128,1024]{2,1,0:T(8,128)(2,1)S(1)} %get-tuple-element.9), channel_id=1, source_target_pairs={{2,0},{4,2},{6,4},{8,6},{10,8},{12,10},{14,12},{16,14},{18,16},{20... | collective-permute-start | bytes 1572872 | tf_op jit(solution)/shard_map/ppermute | solution.py:16
  136.6 30.6 %collective-permute-start.9 = (bf16[2,128,1024]{2,1,0:T(8,128)(2,1)S(1)}, bf16[2,128,1024]{2,1,0:T(8,128)(2,1)S(1)}, u32[]{:S(2)}, u32[]{:S(2)}) collective-permute-start(bf16[2,128,1024]{2,1,0:T(8,128)(2,1)S(1)} %get-tuple-element.10), channel_id=1, source_target_pairs={{2,0},{4,2},{6,4},{8,6},{10,8},{12,10},{14,12},{16,14},{18,16},{20... | collective-permute-start | bytes 1572872 | tf_op jit(solution)/shard_map/ppermute | solution.py:16
  140.5 29.1 %collective-permute-start.8 = (bf16[2,128,1024]{2,1,0:T(8,128)(2,1)S(1)}, bf16[2,128,1024]{2,1,0:T(8,128)(2,1)S(1)}, u32[]{:S(2)}, u32[]{:S(2)}) collective-permute-start(bf16[2,128,1024]{2,1,0:T(8,128)(2,1)S(1)} %get-tuple-element.6), channel_id=1, source_target_pairs={{0,2},{2,4},{4,6},{6,8},{8,10},{10,12},{12,14},{14,16},{16,18},{18... | collective-permute-start | bytes 1572872 | tf_op jit(solution)/shard_map/ppermute | solution.py:16
  144.1 15.2 %collective-permute-start.2 = (bf16[1]{0:T(256)(128)(2,1)}, bf16[1]{0:T(256)(128)(2,1)}, u32[]{:S(2)}, u32[]{:S(2)}) collective-permute-start(bf16[1]{0:T(256)(128)(2,1)} %convert_element_type.149), channel_id=1, source_target_pairs={{0,2},{2,4},{4,6},{6,8},{8,10},{10,12},{12,14},{14,16},{16,18},{18... | collective-permute-start | bytes 14 | tf_op jit(solution)/shard_map/ppermute | solution.py:16
  156.5 4.8 %collective-permute-start.3 = (bf16[1]{0:T(256)(128)(2,1)}, bf16[1]{0:T(256)(128)(2,1)}, u32[]{:S(2)}, u32[]{:S(2)}) collective-permute-start(bf16[1]{0:T(256)(128)(2,1)} %convert_element_type.151), channel_id=1, source_target_pairs={{2,0},{4,2},{6,4},{8,6},{10,8},{12,10},{14,12},{16,14},{18,16},{20... | collective-permute-start | bytes 14 | tf_op jit(solution)/shard_map/ppermute | solution.py:16
  159.3 16.4 %collective-permute-start.7 = (bf16[2,128,1024]{2,1,0:T(8,128)(2,1)S(1)}, bf16[2,128,1024]{2,1,0:T(8,128)(2,1)S(1)}, u32[]{:S(2)}, u32[]{:S(2)}) collective-permute-start(bf16[2,128,1024]{2,1,0:T(8,128)(2,1)S(1)} %get-tuple-element.11), channel_id=1, source_target_pairs={{2,0},{4,2},{6,4},{8,6},{10,8},{12,10},{14,12},{16,14},{18,16},{20... | collective-permute-start | bytes 1572872 | tf_op jit(solution)/shard_map/ppermute | solution.py:16
  161.3 31.3 %collective-permute-start.5 = (bf16[2,128,1024]{2,1,0:T(8,128)(2,1)S(1)}, bf16[2,128,1024]{2,1,0:T(8,128)(2,1)S(1)}, u32[]{:S(2)}, u32[]{:S(2)}) collective-permute-start(bf16[2,128,1024]{2,1,0:T(8,128)(2,1)S(1)} %get-tuple-element.12), channel_id=1, source_target_pairs={{2,0},{4,2},{6,4},{8,6},{10,8},{12,10},{14,12},{16,14},{18,16},{20... | collective-permute-start | bytes 1572872 | tf_op jit(solution)/shard_map/ppermute | solution.py:16
  163.2 29.4 %collective-permute-start = (bf16[2,128,1024]{2,1,0:T(8,128)(2,1)S(1)}, bf16[2,128,1024]{2,1,0:T(8,128)(2,1)S(1)}, u32[]{:S(2)}, u32[]{:S(2)}) collective-permute-start(bf16[2,128,1024]{2,1,0:T(8,128)(2,1)S(1)} %get-tuple-element.5), channel_id=1, source_target_pairs={{0,2},{2,4},{4,6},{6,8},{8,10},{10,12},{12,14},{14,16},{16,18},{18... | collective-permute-start | bytes 1572872 | tf_op jit(solution)/shard_map/ppermute | solution.py:16
  167.2 25.4 %collective-permute-start.6 = (bf16[2,128,1024]{2,1,0:T(8,128)(2,1)S(1)}, bf16[2,128,1024]{2,1,0:T(8,128)(2,1)S(1)}, u32[]{:S(2)}, u32[]{:S(2)}) collective-permute-start(bf16[2,128,1024]{2,1,0:T(8,128)(2,1)S(1)} %get-tuple-element.7), channel_id=1, source_target_pairs={{0,2},{2,4},{4,6},{6,8},{8,10},{10,12},{12,14},{14,16},{16,18},{18... | collective-permute-start | bytes 1572872 | tf_op jit(solution)/shard_map/ppermute | solution.py:16
  169.6 23.0 %collective-permute-start.4 = (bf16[2,128,1024]{2,1,0:T(8,128)(2,1)S(1)}, bf16[2,128,1024]{2,1,0:T(8,128)(2,1)S(1)}, u32[]{:S(2)}, u32[]{:S(2)}) collective-permute-start(bf16[2,128,1024]{2,1,0:T(8,128)(2,1)S(1)} %get-tuple-element.8), channel_id=1, source_target_pairs={{0,2},{2,4},{4,6},{6,8},{8,10},{10,12},{12,14},{14,16},{16,18},{18... | collective-permute-start | bytes 1572872 | tf_op jit(solution)/shard_map/ppermute | solution.py:16
Sparse Core Ops, SparseCore 0:
  8.9 57.7 all-gather.7
  68.2 56.7 all-gather.5
where the time goes:
time: 203 us; the launch traced here: 202 us
  waiting for transfers between devices  129 us (64%)
  starting transfers between devices  37.6 us (19%)
  between operations  16.2 us (8%)
  matrix products  11 us (5%)
  other arithmetic  5.95 us (3%)
  blocking collectives  3.09 us (2%)
    all_gather x1, waiting for transfers between devices, body(): lax.all_gather(tokens[0], 'shard', axis=0, tiled=True)  55.3 us
    all_gather x1, waiting for transfers between devices, body(): lax.all_gather(cotangent[0], 'shard', axis=0, tiled=True)  54.8 us
    ppermute x10, starting transfers between devices, passed_along(): return lax.ppermute(shard, axis, pairs)  37.5 us
    ppermute x10, waiting for transfers between devices, passed_along(): return lax.ppermute(shard, axis, pairs)  17 us
  transfers between devices with their start and end apart: 12, of which 4 were waited for; matrix products, arithmetic and copies ran while one was open for 3% of the time, Pallas kernels for 0%

commit v1 on v0

v1 whole, which is shorter than its diff:
```python
import jax
import jax.numpy as jnp
from jax import lax
from jax.sharding import PartitionSpec as P


SEQS = 8
learn_rate = 1.0
CHUNKS = (1, 1, 2)

NT = (((1,), (1,)), ((), ()))
NN = (((1,), (0,)), ((), ()))


def dot(a, b, dims):
    return lax.dot_general(a, b, dims, preferred_element_type=jnp.float32)


def passed_along(shard, axis, by):
    peers = lax.axis_size(axis)
    pairs = [(i, i + by) for i in range(peers) if 0 <= i + by < peers]
    return lax.ppermute(shard, axis, pairs)


def swapped(shard):
    return lax.ppermute(shard, "shard", [(0, 1), (1, 0)])


def body(w_pair, w_down, tokens, cotangent, seq_ids, msg_left, msg_right, count_left, count_right):
    pair = w_pair[0]
    down = w_down[0]
    tok_own = tokens[0]
    ids = seq_ids[0]
    left_in, right_in = msg_left[0], msg_right[0]
    hidden, width = down.shape
    rows = tok_own.shape[0]
    total_rows = rows * lax.axis_size("shard")
    width_scale = width ** (-0.5)
    batch_scale = total_rows ** (-0.5)
    unit = hidden // sum(CHUNKS)
    bounds, at = [], 0
    for c in CHUNKS:
        bounds.append((at, at + c * unit))
        at += c * unit

    one_hot = (ids[:, None] == jnp.arange(SEQS, dtype=jnp.int32)[None, :]).astype(jnp.float32)
    own_count = jnp.sum(one_hot, axis=0)
    down_par = swapped(down[bounds[0][0] : bounds[0][1]])
    seq_count = own_count + swapped(own_count)
    tok_par = swapped(tok_own)

    cnt_left = passed_along(1 + count_left, "chain", 1)
    cnt_right = passed_along(1 + count_right, "chain", -1)
    total_count = (1 + cnt_left + cnt_right).astype(jnp.float32)

    seq_len = jnp.sum(one_hot * seq_count[None, :], axis=1)
    tok_weight = total_rows / SEQS / seq_len
    tok_weight, total_count = lax.optimization_barrier((tok_weight, total_count))
    scaled_cot = (tok_weight[:, None] * cotangent[0].astype(jnp.float32)).astype(jnp.bfloat16)

    flat_pair = pair.reshape(2 * hidden, width)
    pre_own = dot(flat_pair, tok_own, NT) * width_scale
    gh_own = dot(down, scaled_cot, NT) * width_scale
    pre_par = dot(flat_pair, tok_par, NT) * width_scale

    def grads_pre(pre, gh, lo, hi):
        gate = pre[lo:hi]
        up = pre[hidden + lo : hidden + hi]
        s = jax.nn.sigmoid(gate)
        grad_gate = (gh * up * s * (1.0 + gate * (1.0 - s))).astype(jnp.bfloat16)
        grad_up = (gh * gate * s).astype(jnp.bfloat16)
        return jnp.concatenate([grad_gate, grad_up], axis=0)

    out = jnp.zeros((1,) + pair.shape, jnp.bfloat16)
    waiting = []
    for k, (lo, hi) in enumerate(bounds):
        gh_send = dot(down_par, scaled_cot, NT) * width_scale
        gh_p = swapped(gh_send)
        if k + 1 < len(bounds):
            down_next = down[bounds[k + 1][0] : bounds[k + 1][1]]
            down_next, gh_send = lax.optimization_barrier((down_next, gh_send))
            down_par = swapped(down_next)
        g_own = grads_pre(pre_own, gh_own[lo:hi], lo, hi)
        g_par = grads_pre(pre_par, gh_p, lo, hi)
        grad = dot(g_own, tok_own, NN) + dot(g_par, tok_par, NN)
        grad = grad.reshape(2, hi - lo, width) * batch_scale
        half = pair[:, lo:hi].astype(jnp.float32) - learn_rate * grad
        send_right = (half + left_in[:, lo:hi].astype(jnp.float32)).astype(jnp.bfloat16)
        send_left = (half + right_in[:, lo:hi].astype(jnp.float32)).astype(jnp.bfloat16)
        if k + 1 < len(bounds):
            down_par, send_right, send_left = lax.optimization_barrier(
                (down_par, send_right, send_left)
            )
        recv_left = passed_along(send_right, "chain", 1)
        recv_right = passed_along(send_left, "chain", -1)
        waiting.append((lo, half, recv_left, recv_right))
    for lo, half, recv_left, recv_right in waiting:
        new = (half + recv_left.astype(jnp.float32) + recv_right.astype(jnp.float32)) / total_count
        out = lax.dynamic_update_slice(out, new.astype(jnp.bfloat16)[None], (0, 0, lo, 0))
    return out


def solution(mesh):
    return jax.shard_map(
        body,
        mesh=mesh,
        in_specs=(
            P("chain", None, "shard", None),
            P("chain", "shard", None),
            P("chain", "shard", None),
            P("chain", "shard", None),
            P("chain", "shard"),
            P("chain", None, "shard", None),
            P("chain", None, "shard", None),
            P("chain"),
            P("chain"),
        ),
        out_specs=P("chain", None, "shard", None),
        check_vma=False,
    )
```

time: 203 us -> 137 us (0.67)
  waiting for transfers between devices: 129 us -> 79.2 us
  between operations: 16.2 us -> 2.9 us
  local copies, waits for them, and re-layouts: 0.03 us -> 4.08 us
  blocking collectives: 3.09 us -> 0 us
  starting transfers between devices: 37.6 us -> 35.5 us
    all_gather x2 -> x0, waiting for transfers between devices: 110 us -> none  [the longest x1 55.3 us: body(): lax.all_gather(tokens[0], 'shard', axis=0, tiled=True)]
    ppermute x0 -> x8, waiting for transfers between devices: none -> 43.7 us  [swapped(): return lax.ppermute(shard, 'shard', [(0, 1), (1, 0)])]
    ppermute x10 -> x8, waiting for transfers between devices: 17 us -> 35.5 us  [passed_along(): return lax.ppermute(shard, axis, pairs)]
    ppermute x10 -> x8, starting transfers between devices: 37.5 us -> 28.9 us  [passed_along(): return lax.ppermute(shard, axis, pairs)]
    ppermute x0 -> x8, starting transfers between devices: none -> 6.66 us  [swapped(): return lax.ppermute(shard, 'shard', [(0, 1), (1, 0)])]
    concatenate x3 -> x0, other arithmetic: 3.17 us -> none  [body(): updated = jnp.concatenate(results, axis=2)]
    all_gather x1 -> x0, blocking collectives: 3.09 us -> none  [body(): lax.all_gather(seq_ids[0].astype(jnp.bfloat16), 'shard', axis=0, tiled=True)]
    slice x0 -> x2, local copies, waits for them, and re-layouts: none -> 2.14 us  [the longest x1 1.08 us: body(): down_next = down[bounds[k + 1][0]:bounds[k + 1][1]]]
  transfers between devices with their start and end apart: 12 -> 16, of which waited for: 4 -> 7; matrix products, arithmetic and copies ran while one was open for 3% -> 9% of each run, Pallas kernels for 0% -> 0%
where the time goes in v1:
time: 137 us; the launch traced here: 136 us
  waiting for transfers between devices  79.2 us (58%)
  starting transfers between devices  35.5 us (26%)
  matrix products  9.59 us (7%)
  other arithmetic  4.65 us (3%)
  local copies, waits for them, and re-layouts  4.08 us (3%)
  between operations  2.9 us (2%)
    ppermute x8, waiting for transfers between devices, swapped(): return lax.ppermute(shard, 'shard', [(0, 1), (1, 0)])  43.7 us
    ppermute x8, waiting for transfers between devices, passed_along(): return lax.ppermute(shard, axis, pairs)  35.5 us
    ppermute x8, starting transfers between devices, passed_along(): return lax.ppermute(shard, axis, pairs)  28.9 us
    dot_general x12, matrix products, dot(): return lax.dot_general(a, b, dims, preferred_element_type=jnp.float32)  9.59 us
    ppermute x8, starting transfers between devices, swapped(): return lax.ppermute(shard, 'shard', [(0, 1), (1, 0)])  6.66 us
  transfers between devices with their start and end apart: 16, of which 7 were waited for; matrix products, arithmetic and copies ran while one was open for 9% of the time, Pallas kernels for 0%

profile of v1, /device:TPU:9, one launch (start us, length us, event | category | flops | bytes accessed | tf_op | source)
XLA Modules:
  0.0 135.9 jit_solution(13605353206201790769)
XLA Ops:
  0.0 0.9 convert_reduce_fusion
  0.9 1.3 collective-permute-start
  2.9 4.7 %collective-permute-start.1 = (s32[1]{0:T(128)}, s32[1]{0:T(128)}, u32[]{:S(2)}, u32[]{:S(2)}) collective-permute-start(s32[1]{0:T(128)} %add.99), channel_id=1, source_target_pairs={{0,2},{2,4},{4,6},{6,8},{8,10},{10,12},{12,14},{14,16},{16,18},{18... | collective-permute-start | bytes 20 | tf_op jit(solution)/shard_map/ppermute | solution.py:22
  8.2 2.9 %collective-permute-start.2 = (s32[1]{0:T(128)}, s32[1]{0:T(128)}, u32[]{:S(2)}, u32[]{:S(2)}) collective-permute-start(s32[1]{0:T(128)} %add.101), channel_id=1, source_target_pairs={{2,0},{4,2},{6,4},{8,6},{10,8},{12,10},{14,12},{16,14},{18,16},{20... | collective-permute-start | bytes 20 | tf_op jit(solution)/shard_map/ppermute | solution.py:22
  11.3 1.1 slice_bitcast_fusion.2
  12.4 1.3 collective-permute-start.3
  13.7 1.1 slice_bitcast_fusion
  14.8 2.5 %convolution_multiply_fusion.1 = f32[256,256]{1,0:T(8,128)S(1)} fusion(bf16[256,4096]{1,0:T(8,128)(2,1)} %bitcast.69, bf16[1,256,4096]{2,1,0:T(8,128)(2,1)S(1)} %copy-done), kind=kOutput, calls=%fused_computation.19 | convolution fusion | flops 536936448 | bytes 4456448 | tf_op jit(solution)/shard_map/dot_general | solution.py:16
  18.8 1.0 fusion.13
  20.8 41.5 %collective-permute-done.3 = bf16[32,4096]{1,0:T(8,128)(2,1)S(1)} collective-permute-done((bf16[32,4096]{1,0:T(8,128)(2,1)S(1)}, bf16[32,4096]{1,0:T(8,128)(2,1)S(1)}, u32[]{:S(2)}, u32[]{:S(2)}) %collective-permute-start.3) | collective-permute-done | bytes 262176 | tf_op jit(solution)/shard_map/ppermute | solution.py:26
  62.2 0.8 fusion.16
  63.3 1.2 collective-permute-start.6
  64.5 0.7 convolution_multiply_fusion
  66.4 1.1 copy-done.2
  67.4 0.6 copy-done.3
  68.6 0.8 convolution_multiply_fusion.3
  69.4 1.5 %collective-permute-start.9 = (f32[32,256]{1,0:T(8,128)S(1)}, f32[32,256]{1,0:T(8,128)S(1)}, u32[]{:S(2)}, u32[]{:S(2)}) collective-permute-start(f32[32,256]{1,0:T(8,128)S(1)} %convolution_multiply_fusion.3), channel_id=1, source_target_pairs={{0,1},{1,0},{2,3},{3,2},{4,5},{5,4},{6,7},{7,6},{8,9},{9,8},{10,11... | collective-permute-start | bytes 98312 | tf_op jit(solution)/shard_map/ppermute | solution.py:26
  71.0 6.0 %collective-permute-start.8 = (bf16[2,32,4096]{2,1,0:T(8,128)(2,1)S(1)}, bf16[2,32,4096]{2,1,0:T(8,128)(2,1)S(1)}, u32[]{:S(2)}, u32[]{:S(2)}) collective-permute-start(bf16[2,32,4096]{2,1,0:T(8,128)(2,1)S(1)} %get-tuple-element.18), channel_id=1, source_target_pairs={{2,0},{4,2},{6,4},{8,6},{10,8},{12,10},{14,12},{16,14},{18,16},{20... | collective-permute-start | bytes 1572872 | tf_op jit(solution)/shard_map/ppermute | solution.py:22
  77.0 3.7 %collective-permute-start.7 = (bf16[2,32,4096]{2,1,0:T(8,128)(2,1)S(1)}, bf16[2,32,4096]{2,1,0:T(8,128)(2,1)S(1)}, u32[]{:S(2)}, u32[]{:S(2)}) collective-permute-start(bf16[2,32,4096]{2,1,0:T(8,128)(2,1)S(1)} %get-tuple-element.17), channel_id=1, source_target_pairs={{0,2},{2,4},{4,6},{6,8},{8,10},{10,12},{12,14},{14,16},{16,18},{18... | collective-permute-start | bytes 1572872 | tf_op jit(solution)/shard_map/ppermute | solution.py:22
  81.7 9.9 %collective-permute-done.8 = bf16[2,32,4096]{2,1,0:T(8,128)(2,1)S(1)} collective-permute-done((bf16[2,32,4096]{2,1,0:T(8,128)(2,1)S(1)}, bf16[2,32,4096]{2,1,0:T(8,128)(2,1)S(1)}, u32[]{:S(2)}, u32[]{:S(2)}) %collective-permute-start.8) | collective-permute-done | bytes 524320 | tf_op jit(solution)/shard_map/ppermute | solution.py:22
  91.6 0.6 add_convert_fusion.2
  92.2 1.4 %collective-permute-done.10 = bf16[64,4096]{1,0:T(8,128)(2,1)S(1)} collective-permute-done((bf16[64,4096]{1,0:T(8,128)(2,1)S(1)}, bf16[64,4096]{1,0:T(8,128)(2,1)S(1)}, u32[]{:S(2)}, u32[]{:S(2)}) %collective-permute-start.10) | collective-permute-done | bytes 524320 | tf_op jit(solution)/shard_map/ppermute | solution.py:26
  93.6 0.8 convolution_multiply_fusion.2
  95.3 2.0 %collective-permute-start.12 = (bf16[2,32,4096]{2,1,0:T(8,128)(2,1)S(1)}, bf16[2,32,4096]{2,1,0:T(8,128)(2,1)S(1)}, u32[]{:S(2)}, u32[]{:S(2)}) collective-permute-start(bf16[2,32,4096]{2,1,0:T(8,128)(2,1)S(1)} %get-tuple-element.23), channel_id=1, source_target_pairs={{2,0},{4,2},{6,4},{8,6},{10,8},{12,10},{14,12},{16,14},{18,16},{20... | collective-permute-start | bytes 1572872 | tf_op jit(solution)/shard_map/ppermute | solution.py:22
  97.3 4.1 %collective-permute-start.11 = (bf16[2,32,4096]{2,1,0:T(8,128)(2,1)S(1)}, bf16[2,32,4096]{2,1,0:T(8,128)(2,1)S(1)}, u32[]{:S(2)}, u32[]{:S(2)}) collective-permute-start(bf16[2,32,4096]{2,1,0:T(8,128)(2,1)S(1)} %get-tuple-element.22), channel_id=1, source_target_pairs={{0,2},{2,4},{4,6},{6,8},{8,10},{10,12},{12,14},{14,16},{16,18},{18... | collective-permute-start | bytes 1572872 | tf_op jit(solution)/shard_map/ppermute | solution.py:22
  101.4 0.6 fusion
  102.0 0.7 add_convert_fusion.1
  102.7 1.9 %collective-permute-start.15 = (bf16[2,64,4096]{2,1,0:T(8,128)(2,1)S(1)}, bf16[2,64,4096]{2,1,0:T(8,128)(2,1)S(1)}, u32[]{:S(2)}, u32[]{:S(2)}) collective-permute-start(bf16[2,64,4096]{2,1,0:T(8,128)(2,1)S(1)} %get-tuple-element.26), channel_id=1, source_target_pairs={{2,0},{4,2},{6,4},{8,6},{10,8},{12,10},{14,12},{16,14},{18,16},{20... | collective-permute-start | bytes 3145736 | tf_op jit(solution)/shard_map/ppermute | solution.py:22
  104.6 3.6 %collective-permute-start.14 = (bf16[2,64,4096]{2,1,0:T(8,128)(2,1)S(1)}, bf16[2,64,4096]{2,1,0:T(8,128)(2,1)S(1)}, u32[]{:S(2)}, u32[]{:S(2)}) collective-permute-start(bf16[2,64,4096]{2,1,0:T(8,128)(2,1)S(1)} %get-tuple-element.25), channel_id=1, source_target_pairs={{0,2},{2,4},{4,6},{6,8},{8,10},{10,12},{12,14},{14,16},{16,18},{18... | collective-permute-start | bytes 3145736 | tf_op jit(solution)/shard_map/ppermute | solution.py:22
  108.5 14.7 %collective-permute-done.12 = bf16[2,32,4096]{2,1,0:T(8,128)(2,1)S(1)} collective-permute-done((bf16[2,32,4096]{2,1,0:T(8,128)(2,1)S(1)}, bf16[2,32,4096]{2,1,0:T(8,128)(2,1)S(1)}, u32[]{:S(2)}, u32[]{:S(2)}) %collective-permute-start.12) | collective-permute-done | bytes 524320 | tf_op jit(solution)/shard_map/ppermute | solution.py:22
  123.4 11.0 %collective-permute-done.15 = bf16[2,64,4096]{2,1,0:T(8,128)(2,1)S(1)} collective-permute-done((bf16[2,64,4096]{2,1,0:T(8,128)(2,1)S(1)}, bf16[2,64,4096]{2,1,0:T(8,128)(2,1)S(1)}, u32[]{:S(2)}, u32[]{:S(2)}) %collective-permute-start.15) | collective-permute-done | bytes 1048608 | tf_op jit(solution)/shard_map/ppermute | solution.py:22
  134.4 1.6 %bitcast_dynamic-update-slice_fusion = bf16[1,2,128,4096]{3,2,1,0:T(8,128)(2,1)} fusion(bf16[1,2,128,4096]{3,2,1,0:T(8,128)(2,1)} %copy-done.4, f32[]{:T(128)} %bitcast.14, bf16[2,64,4096]{2,1,0:T(8,128)(2,1)S(1)} %collective-permute-done.15, bf16[2,64,4096]{2,1,0:T(8,128)(2,1)S(1)} %collective-permute-done.14, f32[2,64,4096]{2,1,0:T(8,128)S(1)} %bitcast.63, ...), kind=kLoop, calls=%fused_computation.26 | loop fusion | flops 4194304 | bytes 6291968 | tf_op jit(solution)/shard_map/dynamic_update_slice | solution.py:99
  (45 shorter events, 5.6 us)
Async XLA Ops:
  0.0 14.8 %copy-start = (bf16[1,256,4096]{2,1,0:T(8,128)(2,1)S(1)}, bf16[1,256,4096]{2,1,0:T(8,128)(2,1)}, u32[]{:S(2)}) copy-start(bf16[1,256,4096]{2,1,0:T(8,128)(2,1)} %param.11) | copy-start | bytes 6291460
  0.9 17.7 %collective-permute-start = (f32[8]{0:T(128)S(1)}, f32[8]{0:T(128)S(1)}, u32[]{:S(2)}, u32[]{:S(2)}) collective-permute-start(f32[8]{0:T(128)S(1)} %convert_reduce_fusion), channel_id=1, source_target_pairs={{0,1},{1,0},{2,3},{3,2},{4,5},{5,4},{6,7},{7,6},{8,9},{9,8},{10,11... | collective-permute-start | bytes 104 | tf_op jit(solution)/shard_map/ppermute | solution.py:26
  2.9 14.4 %collective-permute-start.1 = (s32[1]{0:T(128)}, s32[1]{0:T(128)}, u32[]{:S(2)}, u32[]{:S(2)}) collective-permute-start(s32[1]{0:T(128)} %add.99), channel_id=1, source_target_pairs={{0,2},{2,4},{4,6},{6,8},{8,10},{10,12},{12,14},{14,16},{16,18},{18... | collective-permute-start | bytes 20 | tf_op jit(solution)/shard_map/ppermute | solution.py:22
  8.2 9.8 %collective-permute-start.2 = (s32[1]{0:T(128)}, s32[1]{0:T(128)}, u32[]{:S(2)}, u32[]{:S(2)}) collective-permute-start(s32[1]{0:T(128)} %add.101), channel_id=1, source_target_pairs={{2,0},{4,2},{6,4},{8,6},{10,8},{12,10},{14,12},{16,14},{18,16},{20... | collective-permute-start | bytes 20 | tf_op jit(solution)/shard_map/ppermute | solution.py:22
  11.1 53.5 %collective-permute-start.5 = (bf16[256,4096]{1,0:T(8,128)(2,1)}, bf16[256,4096]{1,0:T(8,128)(2,1)S(1)}, u32[]{:S(2)}, u32[]{:S(2)}) collective-permute-start(bf16[256,4096]{1,0:T(8,128)(2,1)} %bitcast.64), channel_id=1, source_target_pairs={{0,1},{1,0},{2,3},{3,2},{4,5},{5,4},{6,7},{7,6},{8,9},{9,8},{10,11... | collective-permute-start | bytes 6291464 | tf_op jit(solution)/shard_map/ppermute | solution.py:26
  12.4 49.8 %collective-permute-start.3 = (bf16[32,4096]{1,0:T(8,128)(2,1)S(1)}, bf16[32,4096]{1,0:T(8,128)(2,1)S(1)}, u32[]{:S(2)}, u32[]{:S(2)}) collective-permute-start(bf16[32,4096]{1,0:T(8,128)(2,1)S(1)} %get-tuple-element.32), channel_id=1, source_target_pairs={{0,1},{1,0},{2,3},{3,2},{4,5},{5,4},{6,7},{7,6},{8,9},{9,8},{10,11... | collective-permute-start | bytes 786440 | tf_op jit(solution)/shard_map/ppermute | solution.py:26
  14.8 3.9 %copy-start.6 = (s32[1,256]{1,0:T(1,128)S(1)}, s32[1,256]{1,0:T(1,128)}, u32[]{:S(2)}) copy-start(s32[1,256]{1,0:T(1,128)} %param.13) | copy-start | bytes 3076
  14.8 4.0 %copy-start.5 = (bf16[1,128,4096]{2,1,0:T(8,128)(2,1)S(1)}, bf16[1,128,4096]{2,1,0:T(8,128)(2,1)}, u32[]{:S(2)}) copy-start(bf16[1,128,4096]{2,1,0:T(8,128)(2,1)} %param.10) | copy-start | bytes 3145732
  14.8 4.0 %copy-start.7 = (bf16[1,256,4096]{2,1,0:T(8,128)(2,1)S(1)}, bf16[1,256,4096]{2,1,0:T(8,128)(2,1)}, u32[]{:S(2)}) copy-start(bf16[1,256,4096]{2,1,0:T(8,128)(2,1)} %param.12) | copy-start | bytes 6291460
  20.7 43.8 %copy-start.1 = (bf16[1,2,128,4096]{3,2,1,0:T(8,128)(2,1)S(1)}, bf16[1,2,128,4096]{3,2,1,0:T(8,128)(2,1)}, u32[]{:S(2)}) copy-start(bf16[1,2,128,4096]{3,2,1,0:T(8,128)(2,1)} %param.9) | copy-start | bytes 6291460
  63.0 2.8 %collective-permute-start.4 = (f32[32,256]{1,0:T(8,128)S(1)}, f32[32,256]{1,0:T(8,128)S(1)}, u32[]{:S(2)}, u32[]{:S(2)}) collective-permute-start(f32[32,256]{1,0:T(8,128)S(1)} %fusion.16), channel_id=1, source_target_pairs={{0,1},{1,0},{2,3},{3,2},{4,5},{5,4},{6,7},{7,6},{8,9},{9,8},{10,11... | collective-permute-start | bytes 98312 | tf_op jit(solution)/shard_map/ppermute | solution.py:26
  63.3 5.3 %collective-permute-start.6 = (bf16[32,4096]{1,0:T(8,128)(2,1)S(1)}, bf16[32,4096]{1,0:T(8,128)(2,1)S(1)}, u32[]{:S(2)}, u32[]{:S(2)}) collective-permute-start(bf16[32,4096]{1,0:T(8,128)(2,1)S(1)} %get-tuple-element.16), channel_id=1, source_target_pairs={{0,1},{1,0},{2,3},{3,2},{4,5},{5,4},{6,7},{7,6},{8,9},{9,8},{10,11... | collective-permute-start | bytes 786440 | tf_op jit(solution)/shard_map/ppermute | solution.py:26
  65.9 1.6 %copy-start.2 = (bf16[1,2,128,4096]{3,2,1,0:T(8,128)(2,1)S(1)}, bf16[1,2,128,4096]{3,2,1,0:T(8,128)(2,1)}, u32[]{:S(2)}) copy-start(bf16[1,2,128,4096]{3,2,1,0:T(8,128)(2,1)} %param.15) | copy-start | bytes 6291460
  65.9 2.2 %copy-start.3 = (bf16[1,2,128,4096]{3,2,1,0:T(8,128)(2,1)S(1)}, bf16[1,2,128,4096]{3,2,1,0:T(8,128)(2,1)}, u32[]{:S(2)}) copy-start(bf16[1,2,128,4096]{3,2,1,0:T(8,128)(2,1)} %param.14) | copy-start | bytes 6291460
  69.4 11.7 %collective-permute-start.9 = (f32[32,256]{1,0:T(8,128)S(1)}, f32[32,256]{1,0:T(8,128)S(1)}, u32[]{:S(2)}, u32[]{:S(2)}) collective-permute-start(f32[32,256]{1,0:T(8,128)S(1)} %convolution_multiply_fusion.3), channel_id=1, source_target_pairs={{0,1},{1,0},{2,3},{3,2},{4,5},{5,4},{6,7},{7,6},{8,9},{9,8},{10,11... | collective-permute-start | bytes 98312 | tf_op jit(solution)/shard_map/ppermute | solution.py:26
  71.0 20.6 %collective-permute-start.8 = (bf16[2,32,4096]{2,1,0:T(8,128)(2,1)S(1)}, bf16[2,32,4096]{2,1,0:T(8,128)(2,1)S(1)}, u32[]{:S(2)}, u32[]{:S(2)}) collective-permute-start(bf16[2,32,4096]{2,1,0:T(8,128)(2,1)S(1)} %get-tuple-element.18), channel_id=1, source_target_pairs={{2,0},{4,2},{6,4},{8,6},{10,8},{12,10},{14,12},{16,14},{18,16},{20... | collective-permute-start | bytes 1572872 | tf_op jit(solution)/shard_map/ppermute | solution.py:22
  77.0 14.6 %collective-permute-start.7 = (bf16[2,32,4096]{2,1,0:T(8,128)(2,1)S(1)}, bf16[2,32,4096]{2,1,0:T(8,128)(2,1)S(1)}, u32[]{:S(2)}, u32[]{:S(2)}) collective-permute-start(bf16[2,32,4096]{2,1,0:T(8,128)(2,1)S(1)} %get-tuple-element.17), channel_id=1, source_target_pairs={{0,2},{2,4},{4,6},{6,8},{8,10},{10,12},{12,14},{14,16},{16,18},{18... | collective-permute-start | bytes 1572872 | tf_op jit(solution)/shard_map/ppermute | solution.py:22
  80.7 12.9 %collective-permute-start.10 = (bf16[64,4096]{1,0:T(8,128)(2,1)S(1)}, bf16[64,4096]{1,0:T(8,128)(2,1)S(1)}, u32[]{:S(2)}, u32[]{:S(2)}) collective-permute-start(bf16[64,4096]{1,0:T(8,128)(2,1)S(1)} %slice_bitcast_fusion), channel_id=1, source_target_pairs={{0,1},{1,0},{2,3},{3,2},{4,5},{5,4},{6,7},{7,6},{8,9},{9,8},{10,11... | collective-permute-start | bytes 1572872 | tf_op jit(solution)/shard_map/ppermute | solution.py:26
  94.4 6.9 %collective-permute-start.13 = (f32[64,256]{1,0:T(8,128)S(1)}, f32[64,256]{1,0:T(8,128)S(1)}, u32[]{:S(2)}, u32[]{:S(2)}) collective-permute-start(f32[64,256]{1,0:T(8,128)S(1)} %convolution_multiply_fusion.2), channel_id=1, source_target_pairs={{0,1},{1,0},{2,3},{3,2},{4,5},{5,4},{6,7},{7,6},{8,9},{9,8},{10,11... | collective-permute-start | bytes 196616 | tf_op jit(solution)/shard_map/ppermute | solution.py:26
  95.3 27.9 %collective-permute-start.12 = (bf16[2,32,4096]{2,1,0:T(8,128)(2,1)S(1)}, bf16[2,32,4096]{2,1,0:T(8,128)(2,1)S(1)}, u32[]{:S(2)}, u32[]{:S(2)}) collective-permute-start(bf16[2,32,4096]{2,1,0:T(8,128)(2,1)S(1)} %get-tuple-element.23), channel_id=1, source_target_pairs={{2,0},{4,2},{6,4},{8,6},{10,8},{12,10},{14,12},{16,14},{18,16},{20... | collective-permute-start | bytes 1572872 | tf_op jit(solution)/shard_map/ppermute | solution.py:22
  97.3 25.9 %collective-permute-start.11 = (bf16[2,32,4096]{2,1,0:T(8,128)(2,1)S(1)}, bf16[2,32,4096]{2,1,0:T(8,128)(2,1)S(1)}, u32[]{:S(2)}, u32[]{:S(2)}) collective-permute-start(bf16[2,32,4096]{2,1,0:T(8,128)(2,1)S(1)} %get-tuple-element.22), channel_id=1, source_target_pairs={{0,2},{2,4},{4,6},{6,8},{8,10},{10,12},{12,14},{14,16},{16,18},{18... | collective-permute-start | bytes 1572872 | tf_op jit(solution)/shard_map/ppermute | solution.py:22
  102.7 31.7 %collective-permute-start.15 = (bf16[2,64,4096]{2,1,0:T(8,128)(2,1)S(1)}, bf16[2,64,4096]{2,1,0:T(8,128)(2,1)S(1)}, u32[]{:S(2)}, u32[]{:S(2)}) collective-permute-start(bf16[2,64,4096]{2,1,0:T(8,128)(2,1)S(1)} %get-tuple-element.26), channel_id=1, source_target_pairs={{2,0},{4,2},{6,4},{8,6},{10,8},{12,10},{14,12},{16,14},{18,16},{20... | collective-permute-start | bytes 3145736 | tf_op jit(solution)/shard_map/ppermute | solution.py:22
  104.6 29.8 %collective-permute-start.14 = (bf16[2,64,4096]{2,1,0:T(8,128)(2,1)S(1)}, bf16[2,64,4096]{2,1,0:T(8,128)(2,1)S(1)}, u32[]{:S(2)}, u32[]{:S(2)}) collective-permute-start(bf16[2,64,4096]{2,1,0:T(8,128)(2,1)S(1)} %get-tuple-element.25), channel_id=1, source_target_pairs={{0,2},{2,4},{4,6},{6,8},{8,10},{10,12},{12,14},{14,16},{16,18},{18... | collective-permute-start | bytes 3145736 | tf_op jit(solution)/shard_map/ppermute | solution.py:22
  123.4 11.0 %copy-start.4 = (bf16[1,2,128,4096]{3,2,1,0:T(8,128)(2,1)}, bf16[1,2,128,4096]{3,2,1,0:T(8,128)(2,1)S(1)}, u32[]{:S(2)}) copy-start(bf16[1,2,128,4096]{3,2,1,0:T(8,128)(2,1)S(1)} %bitcast_dynamic-update-slice_fusion.1) | copy-start | bytes 6291460

commit v2 on v1

--- a/solution.py
+++ b/solution.py
@@ -6,7 +6,7 @@
 
 SEQS = 8
 learn_rate = 1.0
-CHUNKS = (1, 1, 2)
+CHUNKS = (1, 1, 1, 1)
 
 NT = (((1,), (1,)), ((), ()))
 NN = (((1,), (0,)), ((), ()))
@@ -16,10 +16,10 @@
     return lax.dot_general(a, b, dims, preferred_element_type=jnp.float32)
 
 
-def passed_along(shard, axis, by):
-    peers = lax.axis_size(axis)
-    pairs = [(i, i + by) for i in range(peers) if 0 <= i + by < peers]
-    return lax.ppermute(shard, axis, pairs)
+def paired(shard, first):
+    peers = lax.axis_size("chain")
+    lows = range(first, peers - 1, 2)
+    return lax.ppermute(shard, "chain", [p for i in lows for p in ((i, i + 1), (i + 1, i))])
 
 
 def swapped(shard):
@@ -47,21 +47,31 @@
     own_count = jnp.sum(one_hot, axis=0)
     down_par = swapped(down[bounds[0][0] : bounds[0][1]])
     seq_count = own_count + swapped(own_count)
-    tok_par = swapped(tok_own)
+    cut = rows // 2
+    tok_a = swapped(tok_own[:cut])
+    tok_b = swapped(tok_own[cut:])
 
-    cnt_left = passed_along(1 + count_left, "chain", 1)
-    cnt_right = passed_along(1 + count_right, "chain", -1)
-    total_count = (1 + cnt_left + cnt_right).astype(jnp.float32)
+    odd = lax.axis_index("chain") % 2 == 1
+    count_far = 1 + jnp.where(odd, count_left, count_right)
+    count_near = 1 + jnp.where(odd, count_right, count_left)
+    cnt_far = paired(count_far, 1)
+    cnt_near = paired(count_near, 0)
+    total_count = (1 + cnt_far + cnt_near).astype(jnp.float32)
+    pair_f32 = pair.astype(jnp.float32)
+    base_far = pair_f32 + jnp.where(odd, left_in, right_in).astype(jnp.float32)
+    base_near = pair_f32 + jnp.where(odd, right_in, left_in).astype(jnp.float32)
 
     seq_len = jnp.sum(one_hot * seq_count[None, :], axis=1)
     tok_weight = total_rows / SEQS / seq_len
-    tok_weight, total_count = lax.optimization_barrier((tok_weight, total_count))
+    tok_weight, total_count, base_far, base_near = lax.optimization_barrier(
+        (tok_weight, total_count, base_far, base_near)
+    )
     scaled_cot = (tok_weight[:, None] * cotangent[0].astype(jnp.float32)).astype(jnp.bfloat16)
 
     flat_pair = pair.reshape(2 * hidden, width)
     pre_own = dot(flat_pair, tok_own, NT) * width_scale
     gh_own = dot(down, scaled_cot, NT) * width_scale
-    pre_par = dot(flat_pair, tok_par, NT) * width_scale
+    pre_par = jnp.concatenate([dot(flat_pair, t, NT) for t in (tok_a, tok_b)], 1) * width_scale
 
     def grads_pre(pre, gh, lo, hi):
         gate = pre[lo:hi]
@@ -82,20 +92,22 @@
             down_par = swapped(down_next)
         g_own = grads_pre(pre_own, gh_own[lo:hi], lo, hi)
         g_par = grads_pre(pre_par, gh_p, lo, hi)
-        grad = dot(g_own, tok_own, NN) + dot(g_par, tok_par, NN)
-        grad = grad.reshape(2, hi - lo, width) * batch_scale
-        half = pair[:, lo:hi].astype(jnp.float32) - learn_rate * grad
-        send_right = (half + left_in[:, lo:hi].astype(jnp.float32)).astype(jnp.bfloat16)
-        send_left = (half + right_in[:, lo:hi].astype(jnp.float32)).astype(jnp.bfloat16)
+        grad = (
+            dot(g_own, tok_own, NN)
+            + dot(g_par[:, :cut], tok_a, NN)
+            + dot(g_par[:, cut:], tok_b, NN)
+        )
+        step = learn_rate * (grad.reshape(2, hi - lo, width) * batch_scale)
+        send_far = (base_far[:, lo:hi] - step).astype(jnp.bfloat16)
+        send_near = (base_near[:, lo:hi] - step).astype(jnp.bfloat16)
         if k + 1 < len(bounds):
-            down_par, send_right, send_left = lax.optimization_barrier(
-                (down_par, send_right, send_left)
-            )
-        recv_left = passed_along(send_right, "chain", 1)
-        recv_right = passed_along(send_left, "chain", -1)
-        waiting.append((lo, half, recv_left, recv_right))
-    for lo, half, recv_left, recv_right in waiting:
-        new = (half + recv_left.astype(jnp.float32) + recv_right.astype(jnp.float32)) / total_count
+            down_par, _, _ = lax.optimization_barrier((down_par, send_far, send_near))
+        recv_far = paired(send_far, 1)
+        recv_near = paired(send_near, 0)
+        half = pair[:, lo:hi].astype(jnp.float32) - step
+        waiting.append((lo, half, recv_far, recv_near))
+    for lo, half, recv_far, recv_near in waiting:
+        new = (half + recv_far.astype(jnp.float32) + recv_near.astype(jnp.float32)) / total_count
         out = lax.dynamic_update_slice(out, new.astype(jnp.bfloat16)[None], (0, 0, lo, 0))
     return out
 

time: 137 us -> 136 us (level)
  starting transfers between devices: 35.5 us -> 30.5 us
  waiting for transfers between devices: 79.2 us -> 82.6 us
    ppermute x8 -> x11, waiting for transfers between devices: 43.7 us -> 51.4 us  [swapped(): return lax.ppermute(shard, 'shard', [(0, 1), (1, 0)])]
    ppermute x8 -> x10, starting transfers between devices: 28.9 us -> 22.3 us  [paired(): lax.ppermute(shard, 'chain', [p for i in lows for p in ((i, i + 1), (i +...]
    ppermute x8 -> x10, waiting for transfers between devices: 35.5 us -> 31.2 us  [paired(): lax.ppermute(shard, 'chain', [p for i in lows for p in ((i, i + 1), (i +...]
    ppermute x8 -> x11, starting transfers between devices: 6.66 us -> 8.21 us  [swapped(): return lax.ppermute(shard, 'shard', [(0, 1), (1, 0)])]
    dot_general x12 -> x20, matrix products: 9.59 us -> 10.3 us  [dot(): return lax.dot_general(a, b, dims, preferred_element_type=jnp.float32)]
  transfers between devices with their start and end apart: 16 -> 21, of which waited for: 7 -> 9; matrix products, arithmetic and copies ran while one was open for 9% -> 11% of each run, Pallas kernels for 0% -> 0%
where the time goes in v2:
time: 136 us; the launch traced here: 135 us
  waiting for transfers between devices  82.6 us (61%)
  starting transfers between devices  30.5 us (22%)
  matrix products  10.3 us (8%)
  other arithmetic  5.99 us (4%)
  local copies, waits for them, and re-layouts  3.13 us (2%)
  between operations  2.97 us (2%)
    ppermute x11, waiting for transfers between devices, swapped(): return lax.ppermute(shard, 'shard', [(0, 1), (1, 0)])  51.4 us
    ppermute x10, waiting for transfers between devices, paired(): lax.ppermute(shard, 'chain', [p for i in lows for p in ((i, i + 1), (i +...  31.2 us
    ppermute x10, starting transfers between devices, paired(): lax.ppermute(shard, 'chain', [p for i in lows for p in ((i, i + 1), (i +...  22.3 us
    dot_general x20, matrix products, dot(): return lax.dot_general(a, b, dims, preferred_element_type=jnp.float32)  10.3 us
    ppermute x11, starting transfers between devices, swapped(): return lax.ppermute(shard, 'shard', [(0, 1), (1, 0)])  8.21 us
  transfers between devices with their start and end apart: 21, of which 9 were waited for; matrix products, arithmetic and copies ran while one was open for 11% of the time, Pallas kernels for 0%

profile of v2, /device:TPU:9, one launch (start us, length us, event | category | flops | bytes accessed | tf_op | source)
XLA Modules:
  0.0 135.5 jit_solution(1531733817597307831)
XLA Ops:
  0.0 0.9 convert_reduce_fusion
  0.9 1.3 collective-permute-start
  3.5 4.7 %collective-permute-start.1 = (s32[1]{0:T(128)}, s32[1]{0:T(128)}, u32[]{:S(2)}, u32[]{:S(2)}) collective-permute-start(s32[1]{0:T(128)} %add.125), channel_id=1, source_target_pairs={{2,4},{4,2},{6,8},{8,6},{10,12},{12,10},{14,16},{16,14},{18,20},{2... | collective-permute-start | bytes 20 | tf_op jit(solution)/shard_map/ppermute | solution.py:22
  8.2 1.0 collective-permute-start.2
  9.2 1.3 slice_bitcast_fusion.2
  10.9 1.3 collective-permute-start.6
  12.2 0.7 fusion.21
  13.0 0.8 copy-done.4
  14.5 1.3 convert_add_fusion
  17.5 0.9 fusion.27
  20.1 0.7 fusion.30
  20.8 1.3 collective-permute-start.4
  22.4 18.0 %collective-permute-done.6 = bf16[128,4096]{1,0:T(8,128)(2,1)S(1)} collective-permute-done((bf16[128,4096]{1,0:T(8,128)(2,1)S(1)}, bf16[128,4096]{1,0:T(8,128)(2,1)S(1)}, u32[]{:S(2)}, u32[]{:S(2)}) %collective-permute-start.6) | collective-permute-done | bytes 1048608 | tf_op jit(solution)/shard_map/ppermute | solution.py:26
  40.4 0.7 fusion.94
  41.1 21.8 %collective-permute-done.5 = bf16[128,4096]{1,0:T(8,128)(2,1)S(1)} collective-permute-done((bf16[128,4096]{1,0:T(8,128)(2,1)S(1)}, bf16[128,4096]{1,0:T(8,128)(2,1)S(1)}, u32[]{:S(2)}, u32[]{:S(2)}) %collective-permute-start.5) | collective-permute-done | bytes 1048608 | tf_op jit(solution)/shard_map/ppermute | solution.py:26
  62.9 0.7 fusion.93
  64.5 4.7 %collective-permute-done.9 = bf16[32,4096]{1,0:T(8,128)(2,1)S(1)} collective-permute-done((bf16[32,4096]{1,0:T(8,128)(2,1)S(1)}, bf16[32,4096]{1,0:T(8,128)(2,1)S(1)}, u32[]{:S(2)}, u32[]{:S(2)}) %collective-permute-start.9) | collective-permute-done | bytes 262176 | tf_op jit(solution)/shard_map/ppermute | solution.py:26
  69.2 0.7 convolution_multiply_fusion.2
  70.7 1.3 collective-permute-start.13
  72.0 0.7 collective-permute-done.10
  73.6 4.1 %collective-permute-done.13 = bf16[32,4096]{1,0:T(8,128)(2,1)S(1)} collective-permute-done((bf16[32,4096]{1,0:T(8,128)(2,1)S(1)}, bf16[32,4096]{1,0:T(8,128)(2,1)S(1)}, u32[]{:S(2)}, u32[]{:S(2)}) %collective-permute-start.13) | collective-permute-done | bytes 262176 | tf_op jit(solution)/shard_map/ppermute | solution.py:26
  77.7 0.7 convolution_multiply_fusion.1
  78.4 1.3 collective-permute-start.14
  80.2 5.5 %collective-permute-start.7 = (bf16[2,32,4096]{2,1,0:T(8,128)(2,1)S(1)}, bf16[2,32,4096]{2,1,0:T(8,128)(2,1)S(1)}, u32[]{:S(2)}, u32[]{:S(2)}) collective-permute-start(bf16[2,32,4096]{2,1,0:T(8,128)(2,1)S(1)} %get-tuple-element.39), channel_id=1, source_target_pairs={{2,4},{4,2},{6,8},{8,6},{10,12},{12,10},{14,16},{16,14},{18,20},{2... | collective-permute-start | bytes 1572872 | tf_op jit(solution)/shard_map/ppermute | solution.py:22
  85.8 3.5 %collective-permute-start.11 = (bf16[2,32,4096]{2,1,0:T(8,128)(2,1)S(1)}, bf16[2,32,4096]{2,1,0:T(8,128)(2,1)S(1)}, u32[]{:S(2)}, u32[]{:S(2)}) collective-permute-start(bf16[2,32,4096]{2,1,0:T(8,128)(2,1)S(1)} %get-tuple-element.37), channel_id=1, source_target_pairs={{2,4},{4,2},{6,8},{8,6},{10,12},{12,10},{14,16},{16,14},{18,20},{2... | collective-permute-start | bytes 1572872 | tf_op jit(solution)/shard_map/ppermute | solution.py:22
  90.5 18.9 %collective-permute-done.7 = bf16[2,32,4096]{2,1,0:T(8,128)(2,1)S(1)} collective-permute-done((bf16[2,32,4096]{2,1,0:T(8,128)(2,1)S(1)}, bf16[2,32,4096]{2,1,0:T(8,128)(2,1)S(1)}, u32[]{:S(2)}, u32[]{:S(2)}) %collective-permute-start.7) | collective-permute-done | bytes 524320 | tf_op jit(solution)/shard_map/ppermute | solution.py:22
  109.4 3.8 %collective-permute-start.15 = (bf16[2,32,4096]{2,1,0:T(8,128)(2,1)S(1)}, bf16[2,32,4096]{2,1,0:T(8,128)(2,1)S(1)}, u32[]{:S(2)}, u32[]{:S(2)}) collective-permute-start(bf16[2,32,4096]{2,1,0:T(8,128)(2,1)S(1)} %get-tuple-element.35), channel_id=1, source_target_pairs={{2,4},{4,2},{6,8},{8,6},{10,12},{12,10},{14,16},{16,14},{18,20},{2... | collective-permute-start | bytes 1572872 | tf_op jit(solution)/shard_map/ppermute | solution.py:22
  113.8 0.7 convolution_multiply_fusion
  115.3 2.1 %collective-permute-done.18 = f32[32,256]{1,0:T(8,128)S(1)} collective-permute-done((f32[32,256]{1,0:T(8,128)S(1)}, f32[32,256]{1,0:T(8,128)S(1)}, u32[]{:S(2)}, u32[]{:S(2)}) %collective-permute-start.18) | collective-permute-done | bytes 32800 | tf_op jit(solution)/shard_map/ppermute | solution.py:26
  118.3 3.1 %collective-permute-start.19 = (bf16[2,32,4096]{2,1,0:T(8,128)(2,1)S(1)}, bf16[2,32,4096]{2,1,0:T(8,128)(2,1)S(1)}, u32[]{:S(2)}, u32[]{:S(2)}) collective-permute-start(bf16[2,32,4096]{2,1,0:T(8,128)(2,1)S(1)} %get-tuple-element.29), channel_id=1, source_target_pairs={{2,4},{4,2},{6,8},{8,6},{10,12},{12,10},{14,16},{16,14},{18,20},{2... | collective-permute-start | bytes 1572872 | tf_op jit(solution)/shard_map/ppermute | solution.py:22
  122.2 12.2 %collective-permute-done.19 = bf16[2,32,4096]{2,1,0:T(8,128)(2,1)S(1)} collective-permute-done((bf16[2,32,4096]{2,1,0:T(8,128)(2,1)S(1)}, bf16[2,32,4096]{2,1,0:T(8,128)(2,1)S(1)}, u32[]{:S(2)}, u32[]{:S(2)}) %collective-permute-start.19) | collective-permute-done | bytes 524320 | tf_op jit(solution)/shard_map/ppermute | solution.py:22
  134.4 1.1 bitcast_dynamic-update-slice_fusion
  (70 shorter events, 10.6 us)
Async XLA Ops:
  0.0 10.8 %copy-start = (bf16[1,256,4096]{2,1,0:T(8,128)(2,1)S(1)}, bf16[1,256,4096]{2,1,0:T(8,128)(2,1)}, u32[]{:S(2)}) copy-start(bf16[1,256,4096]{2,1,0:T(8,128)(2,1)} %param.11) | copy-start | bytes 6291460
  0.9 16.4 %collective-permute-start = (f32[8]{0:T(128)S(1)}, f32[8]{0:T(128)S(1)}, u32[]{:S(2)}, u32[]{:S(2)}) collective-permute-start(f32[8]{0:T(128)S(1)} %convert_reduce_fusion), channel_id=1, source_target_pairs={{0,1},{1,0},{2,3},{3,2},{4,5},{5,4},{6,7},{7,6},{8,9},{9,8},{10,11... | collective-permute-start | bytes 104 | tf_op jit(solution)/shard_map/ppermute | solution.py:26
  3.5 12.3 %collective-permute-start.1 = (s32[1]{0:T(128)}, s32[1]{0:T(128)}, u32[]{:S(2)}, u32[]{:S(2)}) collective-permute-start(s32[1]{0:T(128)} %add.125), channel_id=1, source_target_pairs={{2,4},{4,2},{6,8},{8,6},{10,12},{12,10},{14,16},{16,14},{18,20},{2... | collective-permute-start | bytes 20 | tf_op jit(solution)/shard_map/ppermute | solution.py:22
  8.2 8.6 %collective-permute-start.2 = (s32[1]{0:T(128)}, s32[1]{0:T(128)}, u32[]{:S(2)}, u32[]{:S(2)}) collective-permute-start(s32[1]{0:T(128)} %add.127), channel_id=1, source_target_pairs={{0,2},{2,0},{4,6},{6,4},{8,10},{10,8},{12,14},{14,12},{16,18},{18,... | collective-permute-start | bytes 20 | tf_op jit(solution)/shard_map/ppermute | solution.py:22
  10.5 1.8 %copy-start.1 = (bf16[1,2,128,4096]{3,2,1,0:T(8,128)(2,1)S(1)}, bf16[1,2,128,4096]{3,2,1,0:T(8,128)(2,1)}, u32[]{:S(2)}) copy-start(bf16[1,2,128,4096]{3,2,1,0:T(8,128)(2,1)} %param.9) | copy-start | bytes 6291460
  10.5 9.6 %collective-permute-start.3 = (bf16[32,4096]{1,0:T(8,128)(2,1)S(1)}, bf16[32,4096]{1,0:T(8,128)(2,1)S(1)}, u32[]{:S(2)}, u32[]{:S(2)}) collective-permute-start(bf16[32,4096]{1,0:T(8,128)(2,1)S(1)} %get-tuple-element.33), channel_id=1, source_target_pairs={{0,1},{1,0},{2,3},{3,2},{4,5},{5,4},{6,7},{7,6},{8,9},{9,8},{10,11... | collective-permute-start | bytes 786440 | tf_op jit(solution)/shard_map/ppermute | solution.py:26
  10.9 29.5 %collective-permute-start.6 = (bf16[128,4096]{1,0:T(8,128)(2,1)S(1)}, bf16[128,4096]{1,0:T(8,128)(2,1)S(1)}, u32[]{:S(2)}, u32[]{:S(2)}) collective-permute-start(bf16[128,4096]{1,0:T(8,128)(2,1)S(1)} %get-tuple-element.27), channel_id=1, source_target_pairs={{0,1},{1,0},{2,3},{3,2},{4,5},{5,4},{6,7},{7,6},{8,9},{9,8},{10,11... | collective-permute-start | bytes 3145736 | tf_op jit(solution)/shard_map/ppermute | solution.py:26
  12.2 1.6 %copy-start.4 = (bf16[1,2,128,4096]{3,2,1,0:T(8,128)(2,1)S(1)}, bf16[1,2,128,4096]{3,2,1,0:T(8,128)(2,1)}, u32[]{:S(2)}) copy-start(bf16[1,2,128,4096]{3,2,1,0:T(8,128)(2,1)} %param.15) | copy-start | bytes 6291460
  12.2 2.2 %copy-start.5 = (bf16[1,2,128,4096]{3,2,1,0:T(8,128)(2,1)S(1)}, bf16[1,2,128,4096]{3,2,1,0:T(8,128)(2,1)}, u32[]{:S(2)}) copy-start(bf16[1,2,128,4096]{3,2,1,0:T(8,128)(2,1)} %param.14) | copy-start | bytes 6291460
  14.5 2.9 %copy-start.7 = (s32[1,256]{1,0:T(1,128)S(1)}, s32[1,256]{1,0:T(1,128)}, u32[]{:S(2)}) copy-start(s32[1,256]{1,0:T(1,128)} %param.13) | copy-start | bytes 3076
  14.5 3.0 %copy-start.2 = (bf16[1,256,4096]{2,1,0:T(8,128)(2,1)S(1)}, bf16[1,256,4096]{2,1,0:T(8,128)(2,1)}, u32[]{:S(2)}) copy-start(bf16[1,256,4096]{2,1,0:T(8,128)(2,1)} %param.12) | copy-start | bytes 6291460
  14.5 3.0 %copy-start.6 = (bf16[1,128,4096]{2,1,0:T(8,128)(2,1)S(1)}, bf16[1,128,4096]{2,1,0:T(8,128)(2,1)}, u32[]{:S(2)}) copy-start(bf16[1,128,4096]{2,1,0:T(8,128)(2,1)} %param.10) | copy-start | bytes 3145732
  15.8 47.1 %collective-permute-start.5 = (bf16[128,4096]{1,0:T(8,128)(2,1)S(1)}, bf16[128,4096]{1,0:T(8,128)(2,1)S(1)}, u32[]{:S(2)}, u32[]{:S(2)}) collective-permute-start(bf16[128,4096]{1,0:T(8,128)(2,1)S(1)} %get-tuple-element.28), channel_id=1, source_target_pairs={{0,1},{1,0},{2,3},{3,2},{4,5},{5,4},{6,7},{7,6},{8,9},{9,8},{10,11... | collective-permute-start | bytes 3145736 | tf_op jit(solution)/shard_map/ppermute | solution.py:26
  20.8 42.8 %collective-permute-start.4 = (f32[32,256]{1,0:T(8,128)S(1)}, f32[32,256]{1,0:T(8,128)S(1)}, u32[]{:S(2)}, u32[]{:S(2)}) collective-permute-start(f32[32,256]{1,0:T(8,128)S(1)} %fusion.30), channel_id=1, source_target_pairs={{0,1},{1,0},{2,3},{3,2},{4,5},{5,4},{6,7},{7,6},{8,9},{9,8},{10,11... | collective-permute-start | bytes 98312 | tf_op jit(solution)/shard_map/ppermute | solution.py:26
  22.1 47.0 %collective-permute-start.9 = (bf16[32,4096]{1,0:T(8,128)(2,1)S(1)}, bf16[32,4096]{1,0:T(8,128)(2,1)S(1)}, u32[]{:S(2)}, u32[]{:S(2)}) collective-permute-start(bf16[32,4096]{1,0:T(8,128)(2,1)S(1)} %get-tuple-element.19), channel_id=1, source_target_pairs={{0,1},{1,0},{2,3},{3,2},{4,5},{5,4},{6,7},{7,6},{8,9},{9,8},{10,11... | collective-permute-start | bytes 786440 | tf_op jit(solution)/shard_map/ppermute | solution.py:26
  69.9 2.8 %collective-permute-start.10 = (f32[32,256]{1,0:T(8,128)S(1)}, f32[32,256]{1,0:T(8,128)S(1)}, u32[]{:S(2)}, u32[]{:S(2)}) collective-permute-start(f32[32,256]{1,0:T(8,128)S(1)} %convolution_multiply_fusion.2), channel_id=1, source_target_pairs={{0,1},{1,0},{2,3},{3,2},{4,5},{5,4},{6,7},{7,6},{8,9},{9,8},{10,11... | collective-permute-start | bytes 98312 | tf_op jit(solution)/shard_map/ppermute | solution.py:26
  70.7 7.0 %collective-permute-start.13 = (bf16[32,4096]{1,0:T(8,128)(2,1)S(1)}, bf16[32,4096]{1,0:T(8,128)(2,1)S(1)}, u32[]{:S(2)}, u32[]{:S(2)}) collective-permute-start(bf16[32,4096]{1,0:T(8,128)(2,1)S(1)} %get-tuple-element.21), channel_id=1, source_target_pairs={{0,1},{1,0},{2,3},{3,2},{4,5},{5,4},{6,7},{7,6},{8,9},{9,8},{10,11... | collective-permute-start | bytes 786440 | tf_op jit(solution)/shard_map/ppermute | solution.py:26
  78.4 10.9 %collective-permute-start.14 = (f32[32,256]{1,0:T(8,128)S(1)}, f32[32,256]{1,0:T(8,128)S(1)}, u32[]{:S(2)}, u32[]{:S(2)}) collective-permute-start(f32[32,256]{1,0:T(8,128)S(1)} %convolution_multiply_fusion.1), channel_id=1, source_target_pairs={{0,1},{1,0},{2,3},{3,2},{4,5},{5,4},{6,7},{7,6},{8,9},{9,8},{10,11... | collective-permute-start | bytes 98312 | tf_op jit(solution)/shard_map/ppermute | solution.py:26
  80.2 29.2 %collective-permute-start.7 = (bf16[2,32,4096]{2,1,0:T(8,128)(2,1)S(1)}, bf16[2,32,4096]{2,1,0:T(8,128)(2,1)S(1)}, u32[]{:S(2)}, u32[]{:S(2)}) collective-permute-start(bf16[2,32,4096]{2,1,0:T(8,128)(2,1)S(1)} %get-tuple-element.39), channel_id=1, source_target_pairs={{2,4},{4,2},{6,8},{8,6},{10,12},{12,10},{14,16},{16,14},{18,20},{2... | collective-permute-start | bytes 1572872 | tf_op jit(solution)/shard_map/ppermute | solution.py:22
  85.7 27.5 %collective-permute-start.8 = (bf16[2,32,4096]{2,1,0:T(8,128)(2,1)S(1)}, bf16[2,32,4096]{2,1,0:T(8,128)(2,1)S(1)}, u32[]{:S(2)}, u32[]{:S(2)}) collective-permute-start(bf16[2,32,4096]{2,1,0:T(8,128)(2,1)S(1)} %get-tuple-element.40), channel_id=1, source_target_pairs={{0,2},{2,0},{4,6},{6,4},{8,10},{10,8},{12,14},{14,12},{16,18},{18,... | collective-permute-start | bytes 1572872 | tf_op jit(solution)/shard_map/ppermute | solution.py:22
  85.8 29.2 %collective-permute-start.11 = (bf16[2,32,4096]{2,1,0:T(8,128)(2,1)S(1)}, bf16[2,32,4096]{2,1,0:T(8,128)(2,1)S(1)}, u32[]{:S(2)}, u32[]{:S(2)}) collective-permute-start(bf16[2,32,4096]{2,1,0:T(8,128)(2,1)S(1)} %get-tuple-element.37), channel_id=1, source_target_pairs={{2,4},{4,2},{6,8},{8,6},{10,12},{12,10},{14,16},{16,14},{18,20},{2... | collective-permute-start | bytes 1572872 | tf_op jit(solution)/shard_map/ppermute | solution.py:22
  89.3 25.7 %collective-permute-start.12 = (bf16[2,32,4096]{2,1,0:T(8,128)(2,1)S(1)}, bf16[2,32,4096]{2,1,0:T(8,128)(2,1)S(1)}, u32[]{:S(2)}, u32[]{:S(2)}) collective-permute-start(bf16[2,32,4096]{2,1,0:T(8,128)(2,1)S(1)} %get-tuple-element.38), channel_id=1, source_target_pairs={{0,2},{2,0},{4,6},{6,4},{8,10},{10,8},{12,14},{14,12},{16,18},{18,... | collective-permute-start | bytes 1572872 | tf_op jit(solution)/shard_map/ppermute | solution.py:22
  89.4 24.4 %collective-permute-start.17 = (bf16[32,4096]{1,0:T(8,128)(2,1)S(1)}, bf16[32,4096]{1,0:T(8,128)(2,1)S(1)}, u32[]{:S(2)}, u32[]{:S(2)}) collective-permute-start(bf16[32,4096]{1,0:T(8,128)(2,1)S(1)} %get-tuple-element.23), channel_id=1, source_target_pairs={{0,1},{1,0},{2,3},{3,2},{4,5},{5,4},{6,7},{7,6},{8,9},{9,8},{10,11... | collective-permute-start | bytes 786440 | tf_op jit(solution)/shard_map/ppermute | solution.py:26
  109.4 12.5 %collective-permute-start.15 = (bf16[2,32,4096]{2,1,0:T(8,128)(2,1)S(1)}, bf16[2,32,4096]{2,1,0:T(8,128)(2,1)S(1)}, u32[]{:S(2)}, u32[]{:S(2)}) collective-permute-start(bf16[2,32,4096]{2,1,0:T(8,128)(2,1)S(1)} %get-tuple-element.35), channel_id=1, source_target_pairs={{2,4},{4,2},{6,8},{8,6},{10,12},{12,10},{14,16},{16,14},{18,20},{2... | collective-permute-start | bytes 1572872 | tf_op jit(solution)/shard_map/ppermute | solution.py:22
  113.2 8.7 %collective-permute-start.16 = (bf16[2,32,4096]{2,1,0:T(8,128)(2,1)S(1)}, bf16[2,32,4096]{2,1,0:T(8,128)(2,1)S(1)}, u32[]{:S(2)}, u32[]{:S(2)}) collective-permute-start(bf16[2,32,4096]{2,1,0:T(8,128)(2,1)S(1)} %get-tuple-element.36), channel_id=1, source_target_pairs={{0,2},{2,0},{4,6},{6,4},{8,10},{10,8},{12,14},{14,12},{16,18},{18,... | collective-permute-start | bytes 1572872 | tf_op jit(solution)/shard_map/ppermute | solution.py:22
  114.6 2.8 %collective-permute-start.18 = (f32[32,256]{1,0:T(8,128)S(1)}, f32[32,256]{1,0:T(8,128)S(1)}, u32[]{:S(2)}, u32[]{:S(2)}) collective-permute-start(f32[32,256]{1,0:T(8,128)S(1)} %convolution_multiply_fusion), channel_id=1, source_target_pairs={{0,1},{1,0},{2,3},{3,2},{4,5},{5,4},{6,7},{7,6},{8,9},{9,8},{10,11... | collective-permute-start | bytes 98312 | tf_op jit(solution)/shard_map/ppermute | solution.py:26
  118.3 16.1 %collective-permute-start.19 = (bf16[2,32,4096]{2,1,0:T(8,128)(2,1)S(1)}, bf16[2,32,4096]{2,1,0:T(8,128)(2,1)S(1)}, u32[]{:S(2)}, u32[]{:S(2)}) collective-permute-start(bf16[2,32,4096]{2,1,0:T(8,128)(2,1)S(1)} %get-tuple-element.29), channel_id=1, source_target_pairs={{2,4},{4,2},{6,8},{8,6},{10,12},{12,10},{14,16},{16,14},{18,20},{2... | collective-permute-start | bytes 1572872 | tf_op jit(solution)/shard_map/ppermute | solution.py:22
  121.4 13.0 %collective-permute-start.20 = (bf16[2,32,4096]{2,1,0:T(8,128)(2,1)S(1)}, bf16[2,32,4096]{2,1,0:T(8,128)(2,1)S(1)}, u32[]{:S(2)}, u32[]{:S(2)}) collective-permute-start(bf16[2,32,4096]{2,1,0:T(8,128)(2,1)S(1)} %get-tuple-element.30), channel_id=1, source_target_pairs={{0,2},{2,0},{4,6},{6,4},{8,10},{10,8},{12,14},{14,12},{16,18},{18,... | collective-permute-start | bytes 1572872 | tf_op jit(solution)/shard_map/ppermute | solution.py:22
  122.2 12.2 %copy-start.3 = (bf16[1,2,128,4096]{3,2,1,0:T(8,128)(2,1)}, bf16[1,2,128,4096]{3,2,1,0:T(8,128)(2,1)S(1)}, u32[]{:S(2)}) copy-start(bf16[1,2,128,4096]{3,2,1,0:T(8,128)(2,1)S(1)} %bitcast_dynamic-update-slice_fusion.1) | copy-start | bytes 6291460

commit v3 on v2

--- a/solution.py
+++ b/solution.py
@@ -7,6 +7,7 @@
 SEQS = 8
 learn_rate = 1.0
 CHUNKS = (1, 1, 1, 1)
+REMADE = 5
 
 NT = (((1,), (1,)), ((), ()))
 NN = (((1,), (0,)), ((), ()))
@@ -47,9 +48,9 @@
     own_count = jnp.sum(one_hot, axis=0)
     down_par = swapped(down[bounds[0][0] : bounds[0][1]])
     seq_count = own_count + swapped(own_count)
-    cut = rows // 2
-    tok_a = swapped(tok_own[:cut])
-    tok_b = swapped(tok_own[cut:])
+    cut = width * REMADE // 16
+    tok_a = swapped(tok_own[:, :cut])
+    tok_b = swapped(tok_own[:, cut:])
 
     odd = lax.axis_index("chain") % 2 == 1
     count_far = 1 + jnp.where(odd, count_left, count_right)
@@ -60,18 +61,20 @@
     pair_f32 = pair.astype(jnp.float32)
     base_far = pair_f32 + jnp.where(odd, left_in, right_in).astype(jnp.float32)
     base_near = pair_f32 + jnp.where(odd, right_in, left_in).astype(jnp.float32)
+    far_tok_own = paired(tok_own[:, :cut], 1)
+    far_base = paired(base_far[:, :, :cut].astype(jnp.bfloat16), 1)
+    far_tok_par = paired(tok_a, 1)
 
     seq_len = jnp.sum(one_hot * seq_count[None, :], axis=1)
     tok_weight = total_rows / SEQS / seq_len
-    tok_weight, total_count, base_far, base_near = lax.optimization_barrier(
-        (tok_weight, total_count, base_far, base_near)
-    )
     scaled_cot = (tok_weight[:, None] * cotangent[0].astype(jnp.float32)).astype(jnp.bfloat16)
 
     flat_pair = pair.reshape(2 * hidden, width)
     pre_own = dot(flat_pair, tok_own, NT) * width_scale
     gh_own = dot(down, scaled_cot, NT) * width_scale
-    pre_par = jnp.concatenate([dot(flat_pair, t, NT) for t in (tok_a, tok_b)], 1) * width_scale
+    pre_par = (
+        dot(flat_pair[:, :cut], tok_a, NT) + dot(flat_pair[:, cut:], tok_b, NT)
+    ) * width_scale
 
     def grads_pre(pre, gh, lo, hi):
         gate = pre[lo:hi]
@@ -81,34 +84,61 @@
         grad_up = (gh * gate * s).astype(jnp.bfloat16)
         return jnp.concatenate([grad_gate, grad_up], axis=0)
 
+    def step_of(grad, chunk):
+        return learn_rate * (grad.reshape(2, chunk, grad.shape[1]) * batch_scale)
+
     out = jnp.zeros((1,) + pair.shape, jnp.bfloat16)
     waiting = []
+    ends = [down[lo:hi] for lo, hi in bounds]
+    down_par = {0: down_par}
     for k, (lo, hi) in enumerate(bounds):
-        gh_send = dot(down_par, scaled_cot, NT) * width_scale
+        gh_send = dot(down_par[k], scaled_cot, NT) * width_scale
         gh_p = swapped(gh_send)
-        if k + 1 < len(bounds):
-            down_next = down[bounds[k + 1][0] : bounds[k + 1][1]]
-            down_next, gh_send = lax.optimization_barrier((down_next, gh_send))
-            down_par = swapped(down_next)
+        if k == 0:
+            for j in range(1, len(bounds)):
+                down_par[j] = swapped(ends[j])
         g_own = grads_pre(pre_own, gh_own[lo:hi], lo, hi)
         g_par = grads_pre(pre_par, gh_p, lo, hi)
-        grad = (
-            dot(g_own, tok_own, NN)
-            + dot(g_par[:, :cut], tok_a, NN)
-            + dot(g_par[:, cut:], tok_b, NN)
+        step_a = step_of(
+            dot(g_own, tok_own[:, :cut], NN) + dot(g_par, tok_a, NN), hi - lo
         )
-        step = learn_rate * (grad.reshape(2, hi - lo, width) * batch_scale)
-        send_far = (base_far[:, lo:hi] - step).astype(jnp.bfloat16)
-        send_near = (base_near[:, lo:hi] - step).astype(jnp.bfloat16)
+        step_b = step_of(
+            dot(g_own, tok_own[:, cut:], NN) + dot(g_par, tok_b, NN), hi - lo
+        )
+        send_far = (base_far[:, lo:hi, cut:] - step_b).astype(jnp.bfloat16)
+        grads = jnp.concatenate([g_own, g_par], axis=1).reshape(2, hi - lo, total_rows)
+        send_far = jnp.concatenate([send_far, grads], axis=2)
+        send_near = jnp.concatenate(
+            [
+                (base_near[:, lo:hi, :cut] - step_a).astype(jnp.bfloat16),
+                (base_near[:, lo:hi, cut:] - step_b).astype(jnp.bfloat16),
+            ],
+            axis=2,
+        )
         if k + 1 < len(bounds):
-            down_par, _, _ = lax.optimization_barrier((down_par, send_far, send_near))
+            base_near, base_far, _, _, down_par[k + 1] = lax.optimization_barrier(
+                (base_near, base_far, send_near, send_far, down_par[k + 1])
+            )
         recv_far = paired(send_far, 1)
         recv_near = paired(send_near, 0)
-        half = pair[:, lo:hi].astype(jnp.float32) - step
-        waiting.append((lo, half, recv_far, recv_near))
-    for lo, half, recv_far, recv_near in waiting:
-        new = (half + recv_far.astype(jnp.float32) + recv_near.astype(jnp.float32)) / total_count
-        out = lax.dynamic_update_slice(out, new.astype(jnp.bfloat16)[None], (0, 0, lo, 0))
+        half_a = pair[:, lo:hi, :cut].astype(jnp.float32) - step_a
+        half_b = pair[:, lo:hi, cut:].astype(jnp.float32) - step_b
+        waiting.append((lo, hi, half_a, half_b, recv_far, recv_near))
+    for k, (lo, hi, half_a, half_b, recv_far, recv_near) in enumerate(waiting):
+        if k > 0:
+            recv_far, recv_near, out = lax.optimization_barrier((recv_far, recv_near, out))
+        far_grads = recv_far[:, :, width - cut :].reshape(2 * (hi - lo), total_rows)
+        far_step = step_of(
+            dot(far_grads[:, :rows], far_tok_own, NN)
+            + dot(far_grads[:, rows:], far_tok_par, NN),
+            hi - lo,
+        )
+        far_a = (far_base[:, lo:hi].astype(jnp.float32) - far_step).astype(jnp.bfloat16)
+        far_b = recv_far[:, :, : width - cut]
+        near_a, near_b = recv_near[:, :, :cut], recv_near[:, :, cut:]
+        for at, half, far, near in ((cut, half_b, far_b, near_b), (0, half_a, far_a, near_a)):
+            new = (half + far.astype(jnp.float32) + near.astype(jnp.float32)) / total_count
+            out = lax.dynamic_update_slice(out, new.astype(jnp.bfloat16)[None], (0, 0, lo, at))
     return out
 
 

time: 136 us -> 158 us (1.16)
  starting transfers between devices: 30.5 us -> 47.9 us
  matrix products: 10.3 us -> 24.5 us
  waiting for transfers between devices: 82.6 us -> 69 us
  local copies, waits for them, and re-layouts: 3.13 us -> 6.97 us
    ppermute x11, waiting for transfers between devices: 51.4 us -> 34.2 us  [swapped(): return lax.ppermute(shard, 'shard', [(0, 1), (1, 0)])]
    ppermute x10 -> x13, starting transfers between devices: 22.3 us -> 36.8 us  [paired(): lax.ppermute(shard, 'chain', [p for i in lows for p in ((i, i + 1), (i +...]
    dot_general x20 -> x32, matrix products: 10.3 us -> 24.5 us  [dot(): return lax.dot_general(a, b, dims, preferred_element_type=jnp.float32)]
    slice x2 -> x8, local copies, waits for them, and re-layouts: 1.42 us -> 6.2 us  [the longest x1 2.55 us: body(): tok_b = swapped(tok_own[:, cut:])]
    ppermute x10 -> x13, waiting for transfers between devices: 31.2 us -> 34.7 us  [paired(): lax.ppermute(shard, 'chain', [p for i in lows for p in ((i, i + 1), (i +...]
    ppermute x11, starting transfers between devices: 8.21 us -> 11.1 us  [swapped(): return lax.ppermute(shard, 'shard', [(0, 1), (1, 0)])]
  transfers between devices with their start and end apart: 21 -> 24, of which waited for: 9 -> 7; matrix products, arithmetic and copies ran while one was open for 11% -> 20% of each run, Pallas kernels for 0% -> 0%
where the time goes in v3:
time: 158 us; the launch traced here: 157 us
  waiting for transfers between devices  69 us (44%)
  starting transfers between devices  47.9 us (30%)
  matrix products  24.5 us (16%)
  local copies, waits for them, and re-layouts  6.97 us (4%)
  other arithmetic  5.74 us (4%)
  between operations  3.15 us (2%)
    ppermute x13, starting transfers between devices, paired(): lax.ppermute(shard, 'chain', [p for i in lows for p in ((i, i + 1), (i +...  36.8 us
    ppermute x13, waiting for transfers between devices, paired(): lax.ppermute(shard, 'chain', [p for i in lows for p in ((i, i + 1), (i +...  34.7 us
    ppermute x11, waiting for transfers between devices, swapped(): return lax.ppermute(shard, 'shard', [(0, 1), (1, 0)])  34.2 us
    dot_general x32, matrix products, dot(): return lax.dot_general(a, b, dims, preferred_element_type=jnp.float32)  24.5 us
    ppermute x11, starting transfers between devices, swapped(): return lax.ppermute(shard, 'shard', [(0, 1), (1, 0)])  11.1 us
  transfers between devices with their start and end apart: 24, of which 7 were waited for; matrix products, arithmetic and copies ran while one was open for 20% of the time, Pallas kernels for 0%

profile of v3, /device:TPU:9, one launch (start us, length us, event | category | flops | bytes accessed | tf_op | source)
XLA Modules:
  0.0 157.2 jit_solution(8577394785670513676)
XLA Ops:
  0.0 2.1 %slice.338 = bf16[256,1280]{1,0:T(8,128)(2,1)} slice(bf16[256,4096]{1,0:T(8,128)(2,1)} %bitcast.107), slice={[0:256], [0:1280]} | slice | bytes 1310720 | tf_op jit(solution)/shard_map/slice | solution.py:103
  3.4 3.9 %collective-permute-start.22 = (bf16[256,1280]{1,0:T(8,128)(2,1)}, bf16[256,1280]{1,0:T(8,128)(2,1)}, u32[]{:S(2)}, u32[]{:S(2)}) collective-permute-start(bf16[256,1280]{1,0:T(8,128)(2,1)} %slice.338), channel_id=1, source_target_pairs={{2,4},{4,2},{6,8},{8,6},{10,12},{12,10},{14,16},{16,14},{18,20},{2... | collective-permute-start | bytes 1966088 | tf_op jit(solution)/shard_map/ppermute | solution.py:23
  8.4 2.6 %slice.341 = bf16[256,2816]{1,0:T(8,128)(2,1)} slice(bf16[256,4096]{1,0:T(8,128)(2,1)} %bitcast.108), slice={[0:256], [1280:4096]} | slice | bytes 2883584 | tf_op jit(solution)/shard_map/slice | solution.py:53
  13.5 8.7 %collective-permute-start.19 = (s32[1]{0:T(128)}, s32[1]{0:T(128)}, u32[]{:S(2)}, u32[]{:S(2)}) collective-permute-start(s32[1]{0:T(128)} %add.193), channel_id=1, source_target_pairs={{2,4},{4,2},{6,8},{8,6},{10,12},{12,10},{14,16},{16,14},{18,20},{2... | collective-permute-start | bytes 20 | tf_op jit(solution)/shard_map/ppermute | solution.py:23
  22.2 2.5 %convolution_multiply_fusion = f32[256,256]{1,0:T(8,128)S(1)} fusion(bf16[256,4096]{1,0:T(8,128)(2,1)} %bitcast.117, bf16[1,256,4096]{2,1,0:T(8,128)(2,1)S(1)} %copy-done), kind=kOutput, calls=%fused_computation.39 | convolution fusion | flops 536936448 | bytes 4456448 | tf_op jit(solution)/shard_map/dot_general | solution.py:17
  24.7 1.4 slice_bitcast_fusion
  26.7 1.3 convert_add_fusion
  30.6 1.3 collective-permute-start.5
  35.5 19.0 %collective-permute-done.1 = bf16[32,4096]{1,0:T(8,128)(2,1)S(1)} collective-permute-done((bf16[32,4096]{1,0:T(8,128)(2,1)S(1)}, bf16[32,4096]{1,0:T(8,128)(2,1)S(1)}, u32[]{:S(2)}, u32[]{:S(2)}) %collective-permute-start.1) | collective-permute-done | bytes 262176 | tf_op jit(solution)/shard_map/ppermute | solution.py:27
  57.3 1.3 collective-permute-start.2
  58.7 1.5 fusion.21
  60.1 11.9 %collective-permute-done.2 = f32[32,256]{1,0:T(8,128)S(1)} collective-permute-done((f32[32,256]{1,0:T(8,128)S(1)}, f32[32,256]{1,0:T(8,128)S(1)}, u32[]{:S(2)}, u32[]{:S(2)}) %collective-permute-start.2) | collective-permute-done | bytes 32800 | tf_op jit(solution)/shard_map/ppermute | solution.py:27
  72.0 4.5 %collective-permute-start.21 = (bf16[2,128,1280]{2,1,0:T(8,128)(2,1)S(1)}, bf16[2,128,1280]{2,1,0:T(8,128)(2,1)S(1)}, u32[]{:S(2)}, u32[]{:S(2)}) collective-permute-start(bf16[2,128,1280]{2,1,0:T(8,128)(2,1)S(1)} %slice.591), channel_id=1, source_target_pairs={{2,4},{4,2},{6,8},{8,6},{10,12},{12,10},{14,16},{16,14},{18,20},{2... | collective-permute-start | bytes 1966088 | tf_op jit(solution)/shard_map/ppermute | solution.py:23
  77.1 1.3 fusion.7
  79.3 1.3 collective-permute-start.6
  80.9 1.6 %collective-permute-done.6 = f32[32,256]{1,0:T(8,128)S(1)} collective-permute-done((f32[32,256]{1,0:T(8,128)S(1)}, f32[32,256]{1,0:T(8,128)S(1)}, u32[]{:S(2)}, u32[]{:S(2)}) %collective-permute-start.6) | collective-permute-done | bytes 32800 | tf_op jit(solution)/shard_map/ppermute | solution.py:27
  82.5 1.3 fusion.8
  86.8 1.7 %collective-permute-done.8 = f32[32,256]{1,0:T(8,128)S(1)} collective-permute-done((f32[32,256]{1,0:T(8,128)S(1)}, f32[32,256]{1,0:T(8,128)S(1)}, u32[]{:S(2)}, u32[]{:S(2)}) %collective-permute-start.8) | collective-permute-done | bytes 32800 | tf_op jit(solution)/shard_map/ppermute | solution.py:27
  88.5 1.3 fusion.9
  92.8 4.0 %collective-permute-start.23 = (bf16[256,1280]{1,0:T(8,128)(2,1)}, bf16[256,1280]{1,0:T(8,128)(2,1)S(1)}, u32[]{:S(2)}, u32[]{:S(2)}) collective-permute-start(bf16[256,1280]{1,0:T(8,128)(2,1)} %collective-permute-done.3), channel_id=1, source_target_pairs={{2,4},{4,2},{6,8},{8,6},{10,12},{12,10},{14,16},{16,14},{18,20},{2... | collective-permute-start | bytes 1966088 | tf_op jit(solution)/shard_map/ppermute | solution.py:23
  96.8 3.7 %collective-permute-start.17 = (bf16[2,32,3328]{2,1,0:T(8,128)(2,1)S(1)}, bf16[2,32,3328]{2,1,0:T(8,128)(2,1)S(1)}, u32[]{:S(2)}, u32[]{:S(2)}) collective-permute-start(bf16[2,32,3328]{2,1,0:T(8,128)(2,1)S(1)} %pad_maximum_fusion.4), channel_id=1, source_target_pairs={{2,4},{4,2},{6,8},{8,6},{10,12},{12,10},{14,16},{16,14},{18,20},{2... | collective-permute-start | bytes 1277960 | tf_op jit(solution)/shard_map/ppermute | solution.py:23
  100.6 1.3 fusion.10
  102.5 23.4 %collective-permute-done.17 = bf16[2,32,3328]{2,1,0:T(8,128)(2,1)S(1)} collective-permute-done((bf16[2,32,3328]{2,1,0:T(8,128)(2,1)S(1)}, bf16[2,32,3328]{2,1,0:T(8,128)(2,1)S(1)}, u32[]{:S(2)}, u32[]{:S(2)}) %collective-permute-start.17) | collective-permute-done | bytes 426016 | tf_op jit(solution)/shard_map/ppermute | solution.py:23
  125.9 3.6 %collective-permute-start.15 = (bf16[2,32,3328]{2,1,0:T(8,128)(2,1)S(1)}, bf16[2,32,3328]{2,1,0:T(8,128)(2,1)S(1)}, u32[]{:S(2)}, u32[]{:S(2)}) collective-permute-start(bf16[2,32,3328]{2,1,0:T(8,128)(2,1)S(1)} %pad_maximum_fusion.5), channel_id=1, source_target_pairs={{2,4},{4,2},{6,8},{8,6},{10,12},{12,10},{14,16},{16,14},{18,20},{2... | collective-permute-start | bytes 1277960 | tf_op jit(solution)/shard_map/ppermute | solution.py:23
  129.7 1.3 fusion.45
  131.0 1.9 %collective-permute-start.13 = (bf16[2,32,3328]{2,1,0:T(8,128)(2,1)S(1)}, bf16[2,32,3328]{2,1,0:T(8,128)(2,1)S(1)}, u32[]{:S(2)}, u32[]{:S(2)}) collective-permute-start(bf16[2,32,3328]{2,1,0:T(8,128)(2,1)S(1)} %pad_maximum_fusion.6), channel_id=1, source_target_pairs={{2,4},{4,2},{6,8},{8,6},{10,12},{12,10},{14,16},{16,14},{18,20},{2... | collective-permute-start | bytes 1277960 | tf_op jit(solution)/shard_map/ppermute | solution.py:23
  134.2 4.7 %collective-permute-start.11 = (bf16[2,32,3328]{2,1,0:T(8,128)(2,1)S(1)}, bf16[2,32,3328]{2,1,0:T(8,128)(2,1)S(1)}, u32[]{:S(2)}, u32[]{:S(2)}) collective-permute-start(bf16[2,32,3328]{2,1,0:T(8,128)(2,1)S(1)} %pad_maximum_fusion.7), channel_id=1, source_target_pairs={{2,4},{4,2},{6,8},{8,6},{10,12},{12,10},{14,16},{16,14},{18,20},{2... | collective-permute-start | bytes 1277960 | tf_op jit(solution)/shard_map/ppermute | solution.py:23
  139.3 1.3 fusion.42
  141.0 8.6 %collective-permute-done.13 = bf16[2,32,3328]{2,1,0:T(8,128)(2,1)S(1)} collective-permute-done((bf16[2,32,3328]{2,1,0:T(8,128)(2,1)S(1)}, bf16[2,32,3328]{2,1,0:T(8,128)(2,1)S(1)}, u32[]{:S(2)}, u32[]{:S(2)}) %collective-permute-start.13) | collective-permute-done | bytes 426016 | tf_op jit(solution)/shard_map/ppermute | solution.py:23
  149.8 1.3 fusion.39
  151.5 2.7 %collective-permute-done.11 = bf16[2,32,3328]{2,1,0:T(8,128)(2,1)S(1)} collective-permute-done((bf16[2,32,3328]{2,1,0:T(8,128)(2,1)S(1)}, bf16[2,32,3328]{2,1,0:T(8,128)(2,1)S(1)}, u32[]{:S(2)}, u32[]{:S(2)}) %collective-permute-start.11) | collective-permute-done | bytes 426016 | tf_op jit(solution)/shard_map/ppermute | solution.py:23
  154.4 1.8 %fusion.36 = f32[64,1280]{1,0:T(8,128)S(1)} fusion(bf16[256,1280]{1,0:T(8,128)(2,1)} %collective-permute-done.22, bf16[64,512]{1,0:T(8,128)(2,1)S(1)} %bitcast.154), kind=kOutput, calls=%fused_computation.101 | convolution fusion | flops 41943040 | bytes 1015808 | tf_op jit(solution)/shard_map/dot_general | solution.py:17
  (113 shorter events, 23.7 us)
Async XLA Ops:
  0.0 22.2 %copy-start = (bf16[1,256,4096]{2,1,0:T(8,128)(2,1)S(1)}, bf16[1,256,4096]{2,1,0:T(8,128)(2,1)}, u32[]{:S(2)}) copy-start(bf16[1,256,4096]{2,1,0:T(8,128)(2,1)} %param.11) | copy-start | bytes 6291460
  2.1 55.2 %collective-permute-start.3 = (bf16[256,1280]{1,0:T(8,128)(2,1)}, bf16[256,1280]{1,0:T(8,128)(2,1)}, u32[]{:S(2)}, u32[]{:S(2)}) collective-permute-start(bf16[256,1280]{1,0:T(8,128)(2,1)} %slice.338), channel_id=1, source_target_pairs={{0,1},{1,0},{2,3},{3,2},{4,5},{5,4},{6,7},{7,6},{8,9},{9,8},{10,11... | collective-permute-start | bytes 1966088 | tf_op jit(solution)/shard_map/ppermute | solution.py:27
  3.4 126.2 %collective-permute-start.22 = (bf16[256,1280]{1,0:T(8,128)(2,1)}, bf16[256,1280]{1,0:T(8,128)(2,1)}, u32[]{:S(2)}, u32[]{:S(2)}) collective-permute-start(bf16[256,1280]{1,0:T(8,128)(2,1)} %slice.338), channel_id=1, source_target_pairs={{2,4},{4,2},{6,8},{8,6},{10,12},{12,10},{14,16},{16,14},{18,20},{2... | collective-permute-start | bytes 1966088 | tf_op jit(solution)/shard_map/ppermute | solution.py:23
  8.1 22.5 %collective-permute-start = (f32[8]{0:T(128)S(1)}, f32[8]{0:T(128)S(1)}, u32[]{:S(2)}, u32[]{:S(2)}) collective-permute-start(f32[8]{0:T(128)S(1)} %convert_reduce_fusion), channel_id=1, source_target_pairs={{0,1},{1,0},{2,3},{3,2},{4,5},{5,4},{6,7},{7,6},{8,9},{9,8},{10,11... | collective-permute-start | bytes 104 | tf_op jit(solution)/shard_map/ppermute | solution.py:27
  11.0 45.5 %collective-permute-start.4 = (bf16[256,2816]{1,0:T(8,128)(2,1)}, bf16[256,2816]{1,0:T(8,128)(2,1)S(1)}, u32[]{:S(2)}, u32[]{:S(2)}) collective-permute-start(bf16[256,2816]{1,0:T(8,128)(2,1)} %slice.341), channel_id=1, source_target_pairs={{0,1},{1,0},{2,3},{3,2},{4,5},{5,4},{6,7},{7,6},{8,9},{9,8},{10,11... | collective-permute-start | bytes 4325384 | tf_op jit(solution)/shard_map/ppermute | solution.py:27
  13.5 14.6 %collective-permute-start.19 = (s32[1]{0:T(128)}, s32[1]{0:T(128)}, u32[]{:S(2)}, u32[]{:S(2)}) collective-permute-start(s32[1]{0:T(128)} %add.193), channel_id=1, source_target_pairs={{2,4},{4,2},{6,8},{8,6},{10,12},{12,10},{14,16},{16,14},{18,20},{2... | collective-permute-start | bytes 20 | tf_op jit(solution)/shard_map/ppermute | solution.py:23
  22.2 3.9 %copy-start.4 = (bf16[1,2,128,4096]{3,2,1,0:T(8,128)(2,1)S(1)}, bf16[1,2,128,4096]{3,2,1,0:T(8,128)(2,1)}, u32[]{:S(2)}) copy-start(bf16[1,2,128,4096]{3,2,1,0:T(8,128)(2,1)} %param.14) | copy-start | bytes 6291460
  22.2 4.0 %copy-start.5 = (bf16[1,2,128,4096]{3,2,1,0:T(8,128)(2,1)S(1)}, bf16[1,2,128,4096]{3,2,1,0:T(8,128)(2,1)}, u32[]{:S(2)}) copy-start(bf16[1,2,128,4096]{3,2,1,0:T(8,128)(2,1)} %param.15) | copy-start | bytes 6291460
  24.7 2.0 %copy-start.1 = (bf16[1,2,128,4096]{3,2,1,0:T(8,128)(2,1)S(1)}, bf16[1,2,128,4096]{3,2,1,0:T(8,128)(2,1)}, u32[]{:S(2)}) copy-start(bf16[1,2,128,4096]{3,2,1,0:T(8,128)(2,1)} %param.9) | copy-start | bytes 6291460
  26.7 5.3 %copy-start.7 = (s32[1,256]{1,0:T(1,128)S(1)}, s32[1,256]{1,0:T(1,128)}, u32[]{:S(2)}) copy-start(s32[1,256]{1,0:T(1,128)} %param.13) | copy-start | bytes 3076
  26.7 5.4 %copy-start.2 = (bf16[1,256,4096]{2,1,0:T(8,128)(2,1)S(1)}, bf16[1,256,4096]{2,1,0:T(8,128)(2,1)}, u32[]{:S(2)}) copy-start(bf16[1,256,4096]{2,1,0:T(8,128)(2,1)} %param.12) | copy-start | bytes 6291460
  26.7 5.4 %copy-start.6 = (bf16[1,128,4096]{2,1,0:T(8,128)(2,1)S(1)}, bf16[1,128,4096]{2,1,0:T(8,128)(2,1)}, u32[]{:S(2)}) copy-start(bf16[1,128,4096]{2,1,0:T(8,128)(2,1)} %param.10) | copy-start | bytes 3145732
  28.1 1.6 %collective-permute-start.20 = (s32[1]{0:T(128)}, s32[1]{0:T(128)}, u32[]{:S(2)}, u32[]{:S(2)}) collective-permute-start(s32[1]{0:T(128)} %add.195), channel_id=1, source_target_pairs={{0,2},{2,0},{4,6},{6,4},{8,10},{10,8},{12,14},{14,12},{16,18},{18,... | collective-permute-start | bytes 20 | tf_op jit(solution)/shard_map/ppermute | solution.py:23
  29.7 24.8 %collective-permute-start.1 = (bf16[32,4096]{1,0:T(8,128)(2,1)S(1)}, bf16[32,4096]{1,0:T(8,128)(2,1)S(1)}, u32[]{:S(2)}, u32[]{:S(2)}) collective-permute-start(bf16[32,4096]{1,0:T(8,128)(2,1)S(1)} %get-tuple-element.45), channel_id=1, source_target_pairs={{0,1},{1,0},{2,3},{3,2},{4,5},{5,4},{6,7},{7,6},{8,9},{9,8},{10,11... | collective-permute-start | bytes 786440 | tf_op jit(solution)/shard_map/ppermute | solution.py:27
  30.6 47.9 %collective-permute-start.5 = (bf16[32,4096]{1,0:T(8,128)(2,1)S(1)}, bf16[32,4096]{1,0:T(8,128)(2,1)S(1)}, u32[]{:S(2)}, u32[]{:S(2)}) collective-permute-start(bf16[32,4096]{1,0:T(8,128)(2,1)S(1)} %get-tuple-element.44), channel_id=1, source_target_pairs={{0,1},{1,0},{2,3},{3,2},{4,5},{5,4},{6,7},{7,6},{8,9},{9,8},{10,11... | collective-permute-start | bytes 786440 | tf_op jit(solution)/shard_map/ppermute | solution.py:27
  54.5 30.0 %collective-permute-start.7 = (bf16[32,4096]{1,0:T(8,128)(2,1)S(1)}, bf16[32,4096]{1,0:T(8,128)(2,1)S(1)}, u32[]{:S(2)}, u32[]{:S(2)}) collective-permute-start(bf16[32,4096]{1,0:T(8,128)(2,1)S(1)} %get-tuple-element.46), channel_id=1, source_target_pairs={{0,1},{1,0},{2,3},{3,2},{4,5},{5,4},{6,7},{7,6},{8,9},{9,8},{10,11... | collective-permute-start | bytes 786440 | tf_op jit(solution)/shard_map/ppermute | solution.py:27
  56.5 34.0 %collective-permute-start.9 = (bf16[32,4096]{1,0:T(8,128)(2,1)S(1)}, bf16[32,4096]{1,0:T(8,128)(2,1)S(1)}, u32[]{:S(2)}, u32[]{:S(2)}) collective-permute-start(bf16[32,4096]{1,0:T(8,128)(2,1)S(1)} %get-tuple-element.43), channel_id=1, source_target_pairs={{0,1},{1,0},{2,3},{3,2},{4,5},{5,4},{6,7},{7,6},{8,9},{9,8},{10,11... | collective-permute-start | bytes 786440 | tf_op jit(solution)/shard_map/ppermute | solution.py:27
  57.3 14.7 %collective-permute-start.2 = (f32[32,256]{1,0:T(8,128)S(1)}, f32[32,256]{1,0:T(8,128)S(1)}, u32[]{:S(2)}, u32[]{:S(2)}) collective-permute-start(f32[32,256]{1,0:T(8,128)S(1)} %fusion.28), channel_id=1, source_target_pairs={{0,1},{1,0},{2,3},{3,2},{4,5},{5,4},{6,7},{7,6},{8,9},{9,8},{10,11... | collective-permute-start | bytes 98312 | tf_op jit(solution)/shard_map/ppermute | solution.py:27
  72.0 62.1 %collective-permute-start.21 = (bf16[2,128,1280]{2,1,0:T(8,128)(2,1)S(1)}, bf16[2,128,1280]{2,1,0:T(8,128)(2,1)S(1)}, u32[]{:S(2)}, u32[]{:S(2)}) collective-permute-start(bf16[2,128,1280]{2,1,0:T(8,128)(2,1)S(1)} %slice.591), channel_id=1, source_target_pairs={{2,4},{4,2},{6,8},{8,6},{10,12},{12,10},{14,16},{16,14},{18,20},{2... | collective-permute-start | bytes 1966088 | tf_op jit(solution)/shard_map/ppermute | solution.py:23
  79.3 3.1 %collective-permute-start.6 = (f32[32,256]{1,0:T(8,128)S(1)}, f32[32,256]{1,0:T(8,128)S(1)}, u32[]{:S(2)}, u32[]{:S(2)}) collective-permute-start(f32[32,256]{1,0:T(8,128)S(1)} %convolution_multiply_fusion.3), channel_id=1, source_target_pairs={{0,1},{1,0},{2,3},{3,2},{4,5},{5,4},{6,7},{7,6},{8,9},{9,8},{10,11... | collective-permute-start | bytes 98312 | tf_op jit(solution)/shard_map/ppermute | solution.py:27
  85.2 3.2 %collective-permute-start.8 = (f32[32,256]{1,0:T(8,128)S(1)}, f32[32,256]{1,0:T(8,128)S(1)}, u32[]{:S(2)}, u32[]{:S(2)}) collective-permute-start(f32[32,256]{1,0:T(8,128)S(1)} %convolution_multiply_fusion.2), channel_id=1, source_target_pairs={{0,1},{1,0},{2,3},{3,2},{4,5},{5,4},{6,7},{7,6},{8,9},{9,8},{10,11... | collective-permute-start | bytes 98312 | tf_op jit(solution)/shard_map/ppermute | solution.py:27
  91.2 5.6 %collective-permute-start.10 = (f32[32,256]{1,0:T(8,128)S(1)}, f32[32,256]{1,0:T(8,128)S(1)}, u32[]{:S(2)}, u32[]{:S(2)}) collective-permute-start(f32[32,256]{1,0:T(8,128)S(1)} %convolution_multiply_fusion.1), channel_id=1, source_target_pairs={{0,1},{1,0},{2,3},{3,2},{4,5},{5,4},{6,7},{7,6},{8,9},{9,8},{10,11... | collective-permute-start | bytes 98312 | tf_op jit(solution)/shard_map/ppermute | solution.py:27
  92.8 38.2 %collective-permute-start.23 = (bf16[256,1280]{1,0:T(8,128)(2,1)}, bf16[256,1280]{1,0:T(8,128)(2,1)S(1)}, u32[]{:S(2)}, u32[]{:S(2)}) collective-permute-start(bf16[256,1280]{1,0:T(8,128)(2,1)} %collective-permute-done.3), channel_id=1, source_target_pairs={{2,4},{4,2},{6,8},{8,6},{10,12},{12,10},{14,16},{16,14},{18,20},{2... | collective-permute-start | bytes 1966088 | tf_op jit(solution)/shard_map/ppermute | solution.py:23
  96.7 36.4 %collective-permute-start.18 = (bf16[2,32,4096]{2,1,0:T(8,128)(2,1)S(1)}, bf16[2,32,4096]{2,1,0:T(8,128)(2,1)S(1)}, u32[]{:S(2)}, u32[]{:S(2)}) collective-permute-start(bf16[2,32,4096]{2,1,0:T(8,128)(2,1)S(1)} %pad_maximum_fusion), channel_id=1, source_target_pairs={{0,2},{2,0},{4,6},{6,4},{8,10},{10,8},{12,14},{14,12},{16,18},{18,... | collective-permute-start | bytes 1572872 | tf_op jit(solution)/shard_map/ppermute | solution.py:23
  96.8 29.1 %collective-permute-start.17 = (bf16[2,32,3328]{2,1,0:T(8,128)(2,1)S(1)}, bf16[2,32,3328]{2,1,0:T(8,128)(2,1)S(1)}, u32[]{:S(2)}, u32[]{:S(2)}) collective-permute-start(bf16[2,32,3328]{2,1,0:T(8,128)(2,1)S(1)} %pad_maximum_fusion.4), channel_id=1, source_target_pairs={{2,4},{4,2},{6,8},{8,6},{10,12},{12,10},{14,16},{16,14},{18,20},{2... | collective-permute-start | bytes 1277960 | tf_op jit(solution)/shard_map/ppermute | solution.py:23
  125.9 13.0 %collective-permute-start.15 = (bf16[2,32,3328]{2,1,0:T(8,128)(2,1)S(1)}, bf16[2,32,3328]{2,1,0:T(8,128)(2,1)S(1)}, u32[]{:S(2)}, u32[]{:S(2)}) collective-permute-start(bf16[2,32,3328]{2,1,0:T(8,128)(2,1)S(1)} %pad_maximum_fusion.5), channel_id=1, source_target_pairs={{2,4},{4,2},{6,8},{8,6},{10,12},{12,10},{14,16},{16,14},{18,20},{2... | collective-permute-start | bytes 1277960 | tf_op jit(solution)/shard_map/ppermute | solution.py:23
  129.6 9.5 %collective-permute-start.16 = (bf16[2,32,4096]{2,1,0:T(8,128)(2,1)S(1)}, bf16[2,32,4096]{2,1,0:T(8,128)(2,1)S(1)}, u32[]{:S(2)}, u32[]{:S(2)}) collective-permute-start(bf16[2,32,4096]{2,1,0:T(8,128)(2,1)S(1)} %pad_maximum_fusion.1), channel_id=1, source_target_pairs={{0,2},{2,0},{4,6},{6,4},{8,10},{10,8},{12,14},{14,12},{16,18},{18,... | collective-permute-start | bytes 1572872 | tf_op jit(solution)/shard_map/ppermute | solution.py:23
  131.0 18.6 %collective-permute-start.13 = (bf16[2,32,3328]{2,1,0:T(8,128)(2,1)S(1)}, bf16[2,32,3328]{2,1,0:T(8,128)(2,1)S(1)}, u32[]{:S(2)}, u32[]{:S(2)}) collective-permute-start(bf16[2,32,3328]{2,1,0:T(8,128)(2,1)S(1)} %pad_maximum_fusion.6), channel_id=1, source_target_pairs={{2,4},{4,2},{6,8},{8,6},{10,12},{12,10},{14,16},{16,14},{18,20},{2... | collective-permute-start | bytes 1277960 | tf_op jit(solution)/shard_map/ppermute | solution.py:23
  133.2 16.4 %collective-permute-start.14 = (bf16[2,32,4096]{2,1,0:T(8,128)(2,1)S(1)}, bf16[2,32,4096]{2,1,0:T(8,128)(2,1)S(1)}, u32[]{:S(2)}, u32[]{:S(2)}) collective-permute-start(bf16[2,32,4096]{2,1,0:T(8,128)(2,1)S(1)} %pad_maximum_fusion.2), channel_id=1, source_target_pairs={{0,2},{2,0},{4,6},{6,4},{8,10},{10,8},{12,14},{14,12},{16,18},{18,... | collective-permute-start | bytes 1572872 | tf_op jit(solution)/shard_map/ppermute | solution.py:23
  134.2 20.0 %collective-permute-start.11 = (bf16[2,32,3328]{2,1,0:T(8,128)(2,1)S(1)}, bf16[2,32,3328]{2,1,0:T(8,128)(2,1)S(1)}, u32[]{:S(2)}, u32[]{:S(2)}) collective-permute-start(bf16[2,32,3328]{2,1,0:T(8,128)(2,1)S(1)} %pad_maximum_fusion.7), channel_id=1, source_target_pairs={{2,4},{4,2},{6,8},{8,6},{10,12},{12,10},{14,16},{16,14},{18,20},{2... | collective-permute-start | bytes 1277960 | tf_op jit(solution)/shard_map/ppermute | solution.py:23
  139.0 15.2 %collective-permute-start.12 = (bf16[2,32,4096]{2,1,0:T(8,128)(2,1)S(1)}, bf16[2,32,4096]{2,1,0:T(8,128)(2,1)S(1)}, u32[]{:S(2)}, u32[]{:S(2)}) collective-permute-start(bf16[2,32,4096]{2,1,0:T(8,128)(2,1)S(1)} %pad_maximum_fusion.3), channel_id=1, source_target_pairs={{0,2},{2,0},{4,6},{6,4},{8,10},{10,8},{12,14},{14,12},{16,18},{18,... | collective-permute-start | bytes 1572872 | tf_op jit(solution)/shard_map/ppermute | solution.py:23
  154.3 2.1 %copy-start.3 = (bf16[1,2,128,4096]{3,2,1,0:T(8,128)(2,1)}, bf16[1,2,128,4096]{3,2,1,0:T(8,128)(2,1)S(1)}, u32[]{:S(2)}) copy-start(bf16[1,2,128,4096]{3,2,1,0:T(8,128)(2,1)S(1)} %bitcast_dynamic-update-slice_fusion) | copy-start | bytes 6291460
